TPU v7x, 32 devices: a whole 2x2x4 slice. The times are simulated.
32 devices in a mesh: fsdp: 4 (over y, x), tensor: 8 (over z, core).
Axes of the slice: x: 2, y: 2, z: 4, core: 2. Of those that a mesh axis runs over, the one named last changes fastest.
Arguments:
- block_input: bfloat16 [8, 1536, 1152], P('fsdp', 'tensor'), may hold values from -6 to 6
- segment_ids: int32 [8, 1536], P('fsdp'), may hold values from -1 to 15, as said below
- norm_gains: float32 [2, 1152], replicated, may hold values from 0.5 to 1.5
- row_biases: float32 [4, 1152], replicated, may hold values from -0.15 to 0.15
- in_projection: bfloat16 [3, 1152, 1152], P(None, 'fsdp', 'tensor'), may hold values from -0.1875 to 0.1875
- query_value_bias: float32 [2, 1152], P(None, 'tensor'), may hold values from -0.12 to 0.12
- out_projection: bfloat16 [1152, 1152], P('tensor', 'fsdp'), may hold values from -4 to 4
- up_weight: bfloat16 [1152, 4304], P('fsdp', 'tensor'), may hold values from -0.1875 to 0.1875
- unit_bias: bfloat16 [4304], P('tensor'), may hold values from -3 to 3
- down_weight: bfloat16 [4304, 1152], P('tensor', 'fsdp'), may hold values from -0.1875 to 0.1875
- cotangent: bfloat16 [8, 1536, 1152], P('fsdp', 'tensor'), may hold values from -6 to 6
Outputs:
- block_output: bfloat16 [8, 1536, 1152], P('fsdp', 'tensor')
- input_grad: float32 [8, 1536, 1152], P('fsdp', 'tensor')
- norm_gains_grad: float32 [2, 1152], replicated
- row_biases_grad: float32 [4, 1152], replicated
- in_projection_grad: float32 [3, 1152, 1152], P(None, 'fsdp', 'tensor')
- query_value_bias_grad: float32 [2, 1152], P(None, 'tensor')
- out_projection_grad: float32 [1152, 1152], P('tensor', 'fsdp')
- up_weight_grad: float32 [1152, 4304], P('fsdp', 'tensor')
- unit_bias_grad: float32 [4304], P('tensor')
- down_weight_grad: float32 [4304, 1152], P('tensor', 'fsdp')
Inputs may be any that keep to these rules, and one draw needn't show every extreme that they name: `segment_ids`: row block b holds 2 images in order; image j is a run of 729 consecutive rows with the id b * 2 + j, and every other row is padding with the id -1.
All inputs are finite; a program needn't handle non-finite values.
Results may differ from a plain program's by a relative error of at most 0.012.
Values may be sent and summed in bfloat16 or wider, within the bound.
A program may use at most 192 MiB of HBM per device.

v0:
```python
import jax
import jax.numpy as jnp
from jax import lax
from jax.sharding import PartitionSpec as P

DH = 72
IMG_MB = 2


EPS = 1e-06
GELU_C = 0.7978845608028654


def norm_forward(values, norm_gain, norm_shift):
    center = values - jnp.mean(values, axis=-1, keepdims=True)
    factor = lax.rsqrt(jnp.mean(center * center, axis=-1, keepdims=True) + EPS)
    scaled = center * factor
    return (scaled * norm_gain + norm_shift, scaled, factor)


def norm_backward(upstream, scaled, factor, norm_gain):
    inside = upstream * norm_gain
    return factor * (
        inside
        - jnp.mean(inside, axis=-1, keepdims=True)
        - scaled * jnp.mean(inside * scaled, axis=-1, keepdims=True)
    )


def gelu(pre_act):
    return (
        0.5
        * pre_act
        * (1.0 + jnp.tanh(GELU_C * (pre_act + 0.044715 * pre_act * pre_act * pre_act)))
    )


def gelu_back(pre_act, upstream):
    return jax.vjp(gelu, pre_act)[1](upstream)[0]


def product(left, right):
    return jnp.dot(left, right, preferred_element_type=jnp.float32)


def product_left_t(left, right):
    return lax.dot_general(
        left, right, (((0,), (0,)), ((), ())), preferred_element_type=jnp.float32
    )


def product_right_t(left, right):
    return lax.dot_general(
        left, right, (((1,), (1,)), ((), ())), preferred_element_type=jnp.float32
    )


def fetch_forward(in_projection, out_projection, up_weight, down_weight):
    return (
        lax.all_gather(in_projection, "fsdp", axis=1, tiled=True),
        lax.all_gather(out_projection, "fsdp", axis=1, tiled=True),
        lax.all_gather(up_weight, "fsdp", axis=0, tiled=True),
        lax.all_gather(down_weight, "fsdp", axis=1, tiled=True),
    )


def fetch_backward(in_projection, out_projection, up_weight, down_weight):
    return (
        lax.all_gather(in_projection, "fsdp", axis=1, tiled=True),
        lax.all_gather(out_projection, "fsdp", axis=1, tiled=True),
        lax.all_gather(up_weight, "fsdp", axis=0, tiled=True),
        lax.all_gather(down_weight, "fsdp", axis=1, tiled=True),
    )


def attend(queries, key_rows, value_rows, segments):
    rows_count, width = queries.shape
    heads = width // DH
    block = rows_count // IMG_MB
    score_scale = DH ** (-0.5)
    query_blocks = queries.reshape(IMG_MB, block, heads, DH)
    key_three = key_rows.reshape(rows_count, heads, DH)
    value_three = value_rows.reshape(rows_count, heads, DH)
    segment_blocks = segments.reshape(IMG_MB, block)

    def one_block(pieces):
        query_block, block_segments = pieces
        scores = (
            jnp.einsum("qhd,khd->hqk", query_block, key_three, preferred_element_type=jnp.float32)
            * score_scale
        )
        allowed_pairs = (block_segments[:, None] == segments[None, :])[None]
        log_total = jnp.log(
            jnp.sum(jnp.where(allowed_pairs, jnp.exp(scores), 0.0), axis=2, keepdims=True)
        )
        probs = jnp.where(allowed_pairs, jnp.exp(scores - log_total), 0.0).astype(jnp.bfloat16)
        context = jnp.einsum(
            "hqk,khd->qhd", probs, value_three, preferred_element_type=jnp.float32
        ).astype(jnp.bfloat16)
        return (context.reshape(block, width), log_total)

    context, log_total = lax.map(one_block, (query_blocks, segment_blocks))
    return (context.reshape(rows_count, width), log_total)


def attend_back(queries, key_rows, value_rows, context, context_grad, log_total, segments):
    rows_count, width = queries.shape
    heads = width // DH
    block = rows_count // IMG_MB
    score_scale = DH ** (-0.5)
    key_three = key_rows.reshape(rows_count, heads, DH)
    value_three = value_rows.reshape(rows_count, heads, DH)
    pieces = (
        queries.reshape(IMG_MB, block, heads, DH),
        context.reshape(IMG_MB, block, heads, DH),
        context_grad.reshape(IMG_MB, block, heads, DH),
        log_total,
        segments.reshape(IMG_MB, block),
    )

    def one_block(carry, piece):
        key_acc, value_acc = carry
        query_block, context_block, back_block, total_block, block_segments = piece
        scores = (
            jnp.einsum("qhd,khd->hqk", query_block, key_three, preferred_element_type=jnp.float32)
            * score_scale
        )
        allowed_pairs = (block_segments[:, None] == segments[None, :])[None]
        exact = jnp.where(allowed_pairs, jnp.exp(scores - total_block), 0.0)
        probs = exact.astype(jnp.bfloat16)
        value_acc = value_acc + jnp.einsum(
            "hqk,qhd->khd", probs, back_block, preferred_element_type=jnp.float32
        )
        prob_grad = jnp.einsum(
            "qhd,khd->hqk", back_block, value_three, preferred_element_type=jnp.float32
        )
        delta = jnp.einsum(
            "qhd,qhd->hq", back_block, context_block, preferred_element_type=jnp.float32
        )[:, :, None]
        score_grad = (exact * (prob_grad - delta) * score_scale).astype(jnp.bfloat16)
        query_grad = jnp.einsum(
            "hqk,khd->qhd", score_grad, key_three, preferred_element_type=jnp.float32
        )
        key_acc = key_acc + jnp.einsum(
            "hqk,qhd->khd", score_grad, query_block, preferred_element_type=jnp.float32
        )
        return ((key_acc, value_acc), query_grad.reshape(block, width))

    zeros = jnp.zeros((rows_count, heads, DH), jnp.float32)
    (key_grad, value_grad), query_grad = lax.scan(one_block, (zeros, zeros), pieces)
    return (
        query_grad.reshape(rows_count, width),
        key_grad.reshape(rows_count, width),
        value_grad.reshape(rows_count, width),
    )


def on_device(
    block_input,
    segment_ids,
    norm_gains,
    row_biases,
    in_projection,
    query_value_bias,
    out_projection,
    up_weight,
    unit_bias,
    down_weight,
    cotangent,
):
    batches = block_input.shape[0]
    model_width = block_input.shape[2]
    head_cols = in_projection.shape[2]
    unit_cols = up_weight.shape[1]
    tensor_count = lax.axis_size("tensor")
    gains_sum = jnp.zeros((2, model_width), jnp.float32)
    shifts_sum = jnp.zeros((4, model_width), jnp.float32)
    in_sum = jnp.zeros((3, model_width, head_cols), jnp.float32)
    bias_sum = jnp.zeros((2, head_cols), jnp.float32)
    out_sum = jnp.zeros((head_cols, model_width), jnp.float32)
    up_sum = jnp.zeros((model_width, unit_cols), jnp.float32)
    down_sum = jnp.zeros((unit_cols, model_width), jnp.float32)
    unit_sum = jnp.zeros((unit_cols,), jnp.float32)
    output_list = []
    grad_list = []
    for batch in range(batches):
        rows_in = block_input[batch]
        segments = segment_ids[batch]
        grad_rows = cotangent[batch]
        in_whole, out_whole, up_whole, down_whole = fetch_forward(
            in_projection, out_projection, up_weight, down_weight
        )
        input_float = rows_in.astype(jnp.float32)
        first_out, first_scaled, first_factor = norm_forward(
            input_float, norm_gains[0], row_biases[0]
        )
        first_norm = first_out.astype(jnp.bfloat16)
        first_full = lax.all_gather(first_norm, "tensor", axis=0, tiled=True)
        projected = jnp.einsum(
            "rd,kdx->krx", first_full, in_whole, preferred_element_type=jnp.float32
        )
        queries = (projected[0] + query_value_bias[0]).astype(jnp.bfloat16)
        key_rows = projected[1].astype(jnp.bfloat16)
        value_rows = (projected[2] + query_value_bias[1]).astype(jnp.bfloat16)
        context, log_total = attend(queries, key_rows, value_rows, segments)
        attention_part = lax.psum_scatter(
            product(context, out_whole), "tensor", scatter_dimension=0, tiled=True
        )
        residual = input_float + attention_part + row_biases[2]
        second_out, second_scaled, second_factor = norm_forward(
            residual, norm_gains[1], row_biases[1]
        )
        second_norm = second_out.astype(jnp.bfloat16)
        upstream = grad_rows.astype(jnp.float32)
        second_full = lax.all_gather(second_norm, "tensor", axis=0, tiled=True)
        pre_act = product(second_full, up_whole) + unit_bias
        hidden = gelu(pre_act).astype(jnp.bfloat16)
        unit_part = lax.psum_scatter(
            product(hidden, down_whole).astype(jnp.bfloat16),
            "tensor",
            scatter_dimension=0,
            tiled=True,
        ).astype(jnp.float32)
        output_list.append((residual + unit_part + row_biases[3]).astype(jnp.bfloat16))
        in_whole, out_whole, up_whole, down_whole = fetch_backward(
            in_projection, out_projection, up_weight, down_weight
        )
        grad_full = lax.all_gather(grad_rows, "tensor", axis=0, tiled=True)
        down_sum = down_sum + product_left_t(hidden, grad_full)
        pre_grad = gelu_back(pre_act, product_right_t(grad_full, down_whole))
        pre_half = pre_grad.astype(jnp.bfloat16)
        unit_sum = unit_sum + jnp.sum(pre_grad, axis=0)
        up_sum = up_sum + product_left_t(second_full, pre_half)
        second_grad = lax.psum_scatter(
            product_right_t(pre_half, up_whole), "tensor", scatter_dimension=0, tiled=True
        )
        residual_grad = upstream + norm_backward(
            second_grad, second_scaled, second_factor, norm_gains[1]
        )
        residual_half = residual_grad.astype(jnp.bfloat16)
        residual_full = lax.all_gather(residual_half, "tensor", axis=0, tiled=True)
        out_sum = out_sum + product_left_t(context, residual_full)
        context_grad = product_right_t(residual_full, out_whole).astype(jnp.bfloat16)
        query_grad, key_grad, value_grad = attend_back(
            queries, key_rows, value_rows, context, context_grad, log_total, segments
        )
        bias_sum = bias_sum + jnp.stack([jnp.sum(query_grad, axis=0), jnp.sum(value_grad, axis=0)])
        triple_half = jnp.stack(
            [
                query_grad.astype(jnp.bfloat16),
                key_grad.astype(jnp.bfloat16),
                value_grad.astype(jnp.bfloat16),
            ]
        )
        in_sum = in_sum + jnp.einsum(
            "rd,krx->kdx", first_full, triple_half, preferred_element_type=jnp.float32
        )
        first_grad = lax.psum_scatter(
            jnp.einsum("krx,kdx->rd", triple_half, in_whole, preferred_element_type=jnp.float32),
            "tensor",
            scatter_dimension=0,
            tiled=True,
        )
        grad_list.append(
            residual_grad + norm_backward(first_grad, first_scaled, first_factor, norm_gains[0])
        )
        gains_sum = gains_sum + jnp.stack(
            [
                jnp.sum(first_grad * first_scaled, axis=0),
                jnp.sum(second_grad * second_scaled, axis=0),
            ]
        )
        shifts_sum = shifts_sum + jnp.stack(
            [
                jnp.sum(first_grad, axis=0),
                jnp.sum(second_grad, axis=0),
                jnp.sum(residual_grad, axis=0),
                jnp.sum(upstream, axis=0),
            ]
        )
    in_grad, out_grad, up_grad, down_grad = (
        lax.psum_scatter(in_sum, "fsdp", scatter_dimension=1, tiled=True),
        lax.psum_scatter(out_sum, "fsdp", scatter_dimension=1, tiled=True),
        lax.psum_scatter(up_sum, "fsdp", scatter_dimension=0, tiled=True),
        lax.psum_scatter(down_sum, "fsdp", scatter_dimension=1, tiled=True),
    )
    tensor_index = lax.axis_index("tensor")
    bias_wide = lax.dynamic_update_slice(
        jnp.zeros((2, head_cols * tensor_count), jnp.float32),
        bias_sum,
        (jnp.int32(0), tensor_index * head_cols),
    )
    unit_wide = lax.dynamic_update_slice(
        jnp.zeros((unit_cols * tensor_count,), jnp.float32), unit_sum, (tensor_index * unit_cols,)
    )
    gains_total, shifts_total, bias_total, unit_total = lax.psum(
        (gains_sum, shifts_sum, bias_wide, unit_wide), ("fsdp", "tensor")
    )
    bias_grad = lax.dynamic_slice_in_dim(bias_total, tensor_index * head_cols, head_cols, 1)
    unit_grad = lax.dynamic_slice_in_dim(unit_total, tensor_index * unit_cols, unit_cols, 0)
    return (
        jnp.stack(output_list),
        jnp.stack(grad_list),
        gains_total,
        shifts_total,
        in_grad,
        bias_grad,
        out_grad,
        up_grad,
        unit_grad,
        down_grad,
    )


def solution(mesh):
    return jax.shard_map(
        on_device,
        mesh=mesh,
        in_specs=(
            P("fsdp", "tensor", None),
            P("fsdp", None),
            P(),
            P(),
            P(None, "fsdp", "tensor"),
            P(None, "tensor"),
            P("tensor", "fsdp"),
            P("fsdp", "tensor"),
            P("tensor"),
            P("tensor", "fsdp"),
            P("fsdp", "tensor", None),
        ),
        out_specs=(
            P("fsdp", "tensor", None),
            P("fsdp", "tensor", None),
            P(),
            P(),
            P(None, "fsdp", "tensor"),
            P(None, "tensor"),
            P("tensor", "fsdp"),
            P("fsdp", "tensor"),
            P("tensor"),
            P("tensor", "fsdp"),
        ),
        check_vma=False,
    )
```

profile of v0, /device:TPU:0, one launch (start us, length us, event | category | flops | bytes accessed | tf_op | source)
XLA Modules:
  0.0 1204.0 jit_solution(9622381354068464262)
XLA Ops:
  18.8 11.3 all-gather.2
  31.6 20.9 %all_gather.49 = bf16[3,1152,144]{2,0,1:T(4,128)(2,1)S(1)} all-gather(bf16[3,288,144]{2,0,1:T(4,128)(2,1)S(1)} %copy.40), channel_id=1, replica_groups=mesh['fsdp'=4,'tensor'=8] {'fsdp'}, dimensions={1}, use_global_device_ids=true | all-gather | bytes 1244160 | tf_op jit(solution)/shard_map/all_gather | solution.py:60
  52.5 3.2 copy.41
  55.7 5.2 all-gather.14.cloned.1.call-done
  60.8 4.2 fusion.173
  65.2 38.2 %all-gather.22.cloned.1.call-done = bf16[1536,1152]{1,0:T(8,128)(2,1)} async-done(((bf16[192,1152]{1,0:T(8,128)(2,1)}), bf16[1536,1152]{1,0:T(8,128)(2,1)}) %all-gather.22.cloned.1.call-update) | async-done | bytes 3538960 | tf_op jit(solution)/shard_map/all_gather | solution.py:198
  103.4 3.9 fusion.175
  116.7 13.7 %while.54 = (s32[]{:T(128)}, bf16[2,768,144]{1,2,0:T(8,128)(2,1)S(1)}, f32[2,2,768,1]{2,1,3,0:T(2,128)S(1)}, s32[2,768]{1,0:T(2,128)S(1)}, s32[1,1536]{1,0:T(1,1...) while((s32[]{:T(128)}, ...), condition=%wide.region_4.5_spmd, body=%wide.region_2.4_spmd.sunk | while | flops 697281024 | bytes 24247424 | solution.py:102
  117.5 3.1 select_reduce_fusion.4
  120.6 2.8 fusion.262
  124.3 3.1 select_reduce_fusion.4
  127.5 2.8 fusion.262
  131.2 4.2 fusion.174
  137.4 13.8 %while.55 = (s32[]{:T(128)}, bf16[2,768,144]{1,2,0:T(8,128)(2,1)S(1)}, f32[2,2,768,1]{2,1,3,0:T(2,128)S(1)}, s32[2,768]{1,0:T(2,128)S(1)}, s32[1,1536]{1,0:T(1,1...) while((s32[]{:T(128)}, ...), condition=%wide.region_13.14_spmd, body=%wide.region_11.13_spmd.sunk | while | flops 697281024 | bytes 24247424 | solution.py:102
  138.2 3.1 select_reduce_fusion.5
  141.3 2.9 fusion.265
  145.0 3.1 select_reduce_fusion.5
  148.2 2.9 fusion.265
  151.2 4.2 fusion.176
  156.1 55.4 %reduce-scatter.17.cloned.1.call-done = f32[192,1152]{1,0:T(8,128)} async-done(((f32[1536,1152]{1,0:T(8,128)}), f32[192,1152]{1,0:T(8,128)}) %reduce-scatter.17.cloned.1.call-update) | async-done | bytes 884752 | tf_op jit(solution)/shard_map/reduce_scatter | solution.py:206
  211.5 77.8 %reduce-scatter.21.cloned.1.call-done = f32[192,1152]{1,0:T(8,128)} async-done(((f32[1536,1152]{1,0:T(8,128)}), f32[192,1152]{1,0:T(8,128)}) %reduce-scatter.21.cloned.1.call-update) | async-done | bytes 884752 | tf_op jit(solution)/shard_map/reduce_scatter | solution.py:206
  298.6 35.0 %all-gather.24.cloned.1.call-done = bf16[1536,1152]{1,0:T(8,128)(2,1)} async-done(((bf16[192,1152]{1,0:T(8,128)(2,1)}), bf16[1536,1152]{1,0:T(8,128)(2,1)}) %all-gather.24.cloned.1.call-update) | async-done | bytes 3538960 | tf_op jit(solution)/shard_map/all_gather | solution.py:215
  333.6 6.5 convolution_add_fusion.2
  340.1 24.0 %all-gather.20.cloned.1.call-done = bf16[538,1152]{0,1:T(8,128)(2,1)} async-done(((bf16[538,288]{0,1:T(8,128)(2,1)}), bf16[538,1152]{0,1:T(8,128)(2,1)}) %all-gather.20.cloned.1.call-update) | async-done | bytes 1239568 | tf_op jit(solution)/shard_map/all_gather | solution.py:63
  364.1 43.6 %all-gather.32.cloned.1.call-done = bf16[1,1536,1152]{2,1,0:T(8,128)(2,1)} async-done(((bf16[1,192,1152]{2,1,0:T(8,128)(2,1)}), bf16[1,1536,1152]{2,1,0:T(8,128)(2,1)}) %all-gather.32.cloned.1.call-update) | async-done | bytes 3538960 | tf_op jit(solution)/shard_map/all_gather | solution.py:228
  407.7 9.2 fusion.170
  418.1 5.3 fusion.142
  423.7 26.5 %all-gather.16.cloned.1.call-done = bf16[1536,1152]{1,0:T(8,128)(2,1)} async-done(((bf16[192,1152]{1,0:T(8,128)(2,1)}), bf16[1536,1152]{1,0:T(8,128)(2,1)}) %all-gather.16.cloned.1.call-update) | async-done | bytes 3538960 | tf_op jit(solution)/shard_map/all_gather | solution.py:215
  450.2 6.6 convolution_add_fusion.3
  456.8 35.9 %all-gather.30.cloned.1.call-done = bf16[1,1536,1152]{2,1,0:T(8,128)(2,1)} async-done(((bf16[1,192,1152]{2,1,0:T(8,128)(2,1)}), bf16[1,1536,1152]{2,1,0:T(8,128)(2,1)}) %all-gather.30.cloned.1.call-update) | async-done | bytes 3538960 | tf_op jit(solution)/shard_map/all_gather | solution.py:228
  492.7 9.2 fusion.169
  503.0 5.4 fusion.146
  508.7 7.7 convolution_convert_fusion.1
  516.5 7.6 convolution_convert_fusion
  524.2 46.6 %reduce-scatter.29.cloned.1.call-done = f32[192,1152]{1,0:T(8,128)} async-done(((f32[1536,1152]{1,0:T(8,128)}), f32[192,1152]{1,0:T(8,128)}) %reduce-scatter.29.cloned.1.call-update) | async-done | bytes 884752 | tf_op jit(solution)/shard_map/reduce_scatter | solution.py:234
  570.8 77.7 %reduce-scatter.25.cloned.1.call-done = f32[192,1152]{1,0:T(8,128)} async-done(((f32[1536,1152]{1,0:T(8,128)}), f32[192,1152]{1,0:T(8,128)}) %reduce-scatter.25.cloned.1.call-update) | async-done | bytes 884752 | tf_op jit(solution)/shard_map/reduce_scatter | solution.py:234
  653.6 39.3 %reduce-scatter.19.cloned.1.call-done = bf16[192,1152]{1,0:T(8,128)(2,1)} async-done(((bf16[1536,1152]{1,0:T(8,128)(2,1)}), bf16[192,1152]{1,0:T(8,128)(2,1)}) %reduce-scatter.19.cloned.1.call-update) | async-done | bytes 442384 | tf_op jit(solution)/shard_map/reduce_scatter | solution.py:218
  692.9 44.5 %reduce-scatter.23.cloned.1.call-done = bf16[192,1152]{1,0:T(8,128)(2,1)} async-done(((bf16[1536,1152]{1,0:T(8,128)(2,1)}), bf16[192,1152]{1,0:T(8,128)(2,1)}) %reduce-scatter.23.cloned.1.call-update) | async-done | bytes 442384 | tf_op jit(solution)/shard_map/reduce_scatter | solution.py:218
  737.4 4.4 fusion.156
  746.1 37.6 %all-gather.26.cloned.1.call-done = bf16[1536,1152]{1,0:T(8,128)(2,1)} async-done(((bf16[192,1152]{1,0:T(8,128)(2,1)}), bf16[1536,1152]{1,0:T(8,128)(2,1)}) %all-gather.26.cloned.1.call-update) | async-done | bytes 3538960 | tf_op jit(solution)/shard_map/all_gather | solution.py:241
  783.7 3.3 convolution_convert_fusion.3
  789.9 40.6 %while.56 = (s32[]{:T(128)}, f32[1536,2,72]{0,2,1:T(8,128)S(1)}, f32[1536,2,72]{0,2,1:T(8,128)}, f32[2,768,144]{1,2,0:T(8,128)}, bf16[2,768,2,72]{1,3,2,0:T(8,12...) while((s32[]{:T(128)}, f32[1536,2,72]{0,2,1:T(8,128)S(1)}, ...), condition=%wide.region_22.23_spmd.clone, body=%wide.region_21.22_spmd.clone.sunk | while | flops 1727150592 | bytes 81067536 | solution.py:150
  802.4 4.1 multiply_convert_fusion.10
  819.8 2.8 fusion.278
  822.7 4.1 multiply_convert_fusion.10
  830.6 3.4 convolution_convert_fusion.2
  835.1 37.6 %while.57 = (s32[]{:T(128)}, f32[1536,2,72]{0,2,1:T(8,128)S(1)}, f32[1536,2,72]{0,2,1:T(8,128)}, f32[2,768,144]{1,2,0:T(8,128)}, bf16[2,768,2,72]{1,3,2,0:T(8,12...) while((s32[]{:T(128)}, f32[1536,2,72]{0,2,1:T(8,128)S(1)}, ...), condition=%wide.region_30.31_spmd.clone, body=%wide.region_29.30_spmd.clone.sunk | while | flops 1727150592 | bytes 77491600 | solution.py:150
  846.2 4.1 multiply_convert_fusion.11
  862.1 2.8 fusion.292
  864.9 4.1 multiply_convert_fusion.11
  872.7 3.0 fusion.177
  891.3 4.0 copy.70
  895.3 6.3 reshape.415
  901.6 5.2 convolution_bitcast_fusion.3
  908.1 5.2 convolution_bitcast_fusion.2
  913.4 5.6 fusion.144
  919.0 4.8 convolution_add_fusion.1
  924.1 6.6 fusion.77
  930.7 4.8 convolution_add_fusion
  940.4 7.8 reduce-scatter.37.cloned.1.call-done
  953.2 74.2 %reduce-scatter.27.cloned.1.call-done = f32[192,1152]{1,0:T(8,128)} async-done(((f32[1536,1152]{1,0:T(8,128)}), f32[192,1152]{1,0:T(8,128)}) %reduce-scatter.27.cloned.1.call-update) | async-done | bytes 884752 | tf_op jit(solution)/shard_map/reduce_scatter | solution.py:258
  1027.4 77.9 %reduce-scatter.31.cloned.1.call-done = f32[192,1152]{1,0:T(8,128)} async-done(((f32[1536,1152]{1,0:T(8,128)}), f32[192,1152]{1,0:T(8,128)}) %reduce-scatter.31.cloned.1.call-update) | async-done | bytes 884752 | tf_op jit(solution)/shard_map/reduce_scatter | solution.py:258
  1107.7 39.9 %all-reduce = (f32[2,1152]{1,0:T(2,128)}, f32[4,1152]{1,0:T(4,128)}, f32[2,1152]{1,0:T(2,128)S(1)}, f32[4304]{0:T(1024)S(1)}) all-reduce(f32[2,1152]{1,0:T(2,128)S(1)} %maximum_add_fusion.1, f32[4,1152]{1,0:T(4,128)S(1)} %maximum_add_fusion, ...), channel_id=1, replica_groups=mesh['fsdp'=4,'tensor'=8] {'fsdp','tensor'}, use_global_device_ids=true, to_apply=%region_38.39 | all-reduce | flops 13520 | bytes 108160 | tf_op jit(solution)/shard_map/psum | solution.py:296
  1152.4 43.9 %reduce-scatter.35.cloned.1.call-done = f32[538,288]{0,1:T(8,128)} async-done(((f32[538,1152]{0,1:T(8,128)}), f32[538,288]{0,1:T(8,128)}) %reduce-scatter.35.cloned.1.call-update) | async-done | bytes 619792 | tf_op jit(solution)/shard_map/reduce_scatter | solution.py:285
  (480 shorter events, 142.6 us)
Async XLA Ops:
  8.0 9.3 copy-start.91
  8.0 9.5 copy-start.88
  8.0 10.7 copy-start.68
  8.0 23.2 %copy-start.57 = (bf16[3,288,144]{1,2,0:T(8,128)(2,1)S(1)}, bf16[3,288,144]{1,2,0:T(8,128)(2,1)}, u32[]{:S(2)}) copy-start(bf16[3,288,144]{1,2,0:T(8,128)(2,1)} %param.23) | copy-start | bytes 746500
  8.1 52.8 %all-gather.14.cloned.1.call-start = ((), (), s32[]{:S(2)}) async-start(), calls=%async_computation.12 | async-start | bytes 3981312 | tf_op jit(solution)/shard_map/all_gather | solution.py:198
  9.5 9.2 copy-start.76
  9.5 9.2 copy-start.78
  11.1 7.7 copy-start.82
  11.1 7.7 copy-start.84
  12.5 6.3 copy-start.65
  16.5 86.9 %all-gather.22.cloned.1.call-start = ((), (), s32[]{:S(2)}) async-start(), calls=%async_computation.18 | async-start | bytes 3981312 | tf_op jit(solution)/shard_map/all_gather | solution.py:198
  17.3 194.3 %reduce-scatter.17.cloned.1.call-start = ((), (), s32[]{:S(2)}) async-start(), calls=%async_computation.13 | async-start | bytes 7962624 | tf_op jit(solution)/shard_map/reduce_scatter | solution.py:206
  65.0 38.4 %copy-start.34 = (bf16[3,1152,144]{1,2,0:T(8,128)(2,1)S(1)}, bf16[3,1152,144]{1,2,0:T(8,128)(2,1)}, u32[]{:S(2)}) copy-start(bf16[3,1152,144]{1,2,0:T(8,128)(2,1)} %copy.41) | copy-start | bytes 2985988
  116.7 14.5 %copy-start.29 = (bf16[1152,144]{0,1:T(8,128)(2,1)S(1)}, bf16[1152,144]{0,1:T(8,128)(2,1)}, u32[]{:S(2)}) copy-start(bf16[1152,144]{0,1:T(8,128)(2,1)} %reshape.400) | copy-start | bytes 995332
  130.4 5.0 copy-start.6
  130.4 5.0 copy-start.64
  135.4 154.0 %reduce-scatter.21.cloned.1.call-start = ((), (), s32[]{:S(2)}) async-start(), calls=%async_computation.19 | async-start | bytes 7962624 | tf_op jit(solution)/shard_map/reduce_scatter | solution.py:206
  151.1 4.3 copy-start
  151.1 4.3 copy-start.4
  151.1 4.3 copy-start.8
  155.5 133.9 %copy-start.2 = (bf16[2,192,1152]{2,1,0:T(8,128)(2,1)S(1)}, bf16[2,192,1152]{2,1,0:T(8,128)(2,1)}, u32[]{:S(2)}) copy-start(bf16[2,192,1152]{2,1,0:T(8,128)(2,1)} %param.19) | copy-start | bytes 2654212
  155.5 136.2 %copy-start.67 = (f32[1152]{0:T(1024)S(1)}, f32[1152]{0:T(1024)}, u32[]{:S(2)}) copy-start(f32[1152]{0:T(1024)} %get-tuple-element.414) | copy-start | bytes 13828
  155.5 143.1 %all-gather.18.cloned.1.call-start = ((), (), s32[]{:S(2)}) async-start(), calls=%async_computation.15 | async-start | bytes 1843200 | tf_op jit(solution)/shard_map/all_gather | solution.py:62
  156.1 177.5 %all-gather.24.cloned.1.call-start = ((), (), s32[]{:S(2)}) async-start(), calls=%async_computation.20 | async-start | bytes 3981312 | tf_op jit(solution)/shard_map/all_gather | solution.py:215
  293.7 70.4 %all-gather.20.cloned.1.call-start = ((), (), s32[]{:S(2)}) async-start(), calls=%async_computation.16 | async-start | bytes 1843200 | tf_op jit(solution)/shard_map/all_gather | solution.py:63
  294.3 113.4 %all-gather.32.cloned.1.call-start = ((), (), s32[]{:S(2)}) async-start(), calls=%async_computation.31 | async-start | bytes 3981312 | tf_op jit(solution)/shard_map/all_gather | solution.py:228
  295.4 154.8 %all-gather.16.cloned.1.call-start = ((), (), s32[]{:S(2)}) async-start(), calls=%async_computation.14 | async-start | bytes 3981312 | tf_op jit(solution)/shard_map/all_gather | solution.py:215
  296.1 196.6 %all-gather.30.cloned.1.call-start = ((), (), s32[]{:S(2)}) async-start(), calls=%async_computation.30 | async-start | bytes 3981312 | tf_op jit(solution)/shard_map/all_gather | solution.py:228
  296.8 274.0 %reduce-scatter.29.cloned.1.call-start = ((), (), s32[]{:S(2)}) async-start(), calls=%async_computation.25 | async-start | bytes 7962624 | tf_op jit(solution)/shard_map/reduce_scatter | solution.py:234
  407.7 10.4 copy-start.96
  423.5 225.1 %reduce-scatter.25.cloned.1.call-start = ((), (), s32[]{:S(2)}) async-start(), calls=%async_computation.22 | async-start | bytes 7962624 | tf_op jit(solution)/shard_map/reduce_scatter | solution.py:234
  492.7 10.4 copy-start.97
  508.4 184.5 %reduce-scatter.19.cloned.1.call-start = ((), (), s32[]{:S(2)}) async-start(), calls=%async_computation.17 | async-start | bytes 3981312 | tf_op jit(solution)/shard_map/reduce_scatter | solution.py:218
  516.4 221.0 %reduce-scatter.23.cloned.1.call-start = ((), (), s32[]{:S(2)}) async-start(), calls=%async_computation.21 | async-start | bytes 3981312 | tf_op jit(solution)/shard_map/reduce_scatter | solution.py:218
  524.1 259.6 %all-gather.26.cloned.1.call-start = ((), (), s32[]{:S(2)}) async-start(), calls=%async_computation.23 | async-start | bytes 3981312 | tf_op jit(solution)/shard_map/all_gather | solution.py:241
  741.8 41.9 %copy-start.30 = (bf16[1152,144]{0,1:T(8,128)(2,1)S(1)}, bf16[1152,144]{0,1:T(8,128)(2,1)}, u32[]{:S(2)}) copy-start(bf16[1152,144]{0,1:T(8,128)(2,1)} %reshape.400) | copy-start | bytes 995332
  743.6 87.0 %all-gather.28.cloned.1.call-start = ((), (), s32[]{:S(2)}) async-start(), calls=%async_computation.26 | async-start | bytes 3981312 | tf_op jit(solution)/shard_map/all_gather | solution.py:241
  745.7 192.9 %reduce-scatter.39.cloned.1.call-start = ((), (), s32[]{:S(2)}) async-start(), calls=%async_computation.33 | async-start | bytes 1474560
  830.5 4.5 copy-start.1
  830.5 4.5 copy-start.42
  830.5 4.5 copy-start.60
  830.5 4.5 copy-start.63
  876.1 4.5 copy-start.25
  880.2 68.0 %reduce-scatter.37.cloned.1.call-start = ((), (), s32[]{:S(2)}) async-start(), calls=%async_computation.32 | async-start | bytes 2949120
  883.7 5.5 copy-start.47
  884.4 4.7 copy-start.49
  895.2 6.3 copy-start.35
  895.2 6.4 copy-start.55
  901.5 125.9 %reduce-scatter.27.cloned.1.call-start = ((), (), s32[]{:S(2)}) async-start(), calls=%async_computation.24 | async-start | bytes 7962624 | tf_op jit(solution)/shard_map/reduce_scatter | solution.py:258
  906.8 198.5 %reduce-scatter.31.cloned.1.call-start = ((), (), s32[]{:S(2)}) async-start(), calls=%async_computation.27 | async-start | bytes 7962624 | tf_op jit(solution)/shard_map/reduce_scatter | solution.py:258
  913.3 5.7 copy-start.99
  913.3 239.0 %reduce-scatter.33.cloned.1.call-start = ((), (), s32[]{:S(2)}) async-start(), calls=%async_computation.28 | async-start | bytes 3686400 | tf_op jit(solution)/shard_map/reduce_scatter | solution.py:284
  913.4 5.7 copy-start.94
  923.9 272.4 %reduce-scatter.35.cloned.1.call-start = ((), (), s32[]{:S(2)}) async-start(), calls=%async_computation.29 | async-start | bytes 3686400 | tf_op jit(solution)/shard_map/reduce_scatter | solution.py:285
  924.1 6.6 copy-start.95
  924.1 6.6 copy-start.101
  936.7 168.7 %copy-start.3 = (bf16[2,192,1152]{2,1,0:T(8,128)(2,1)S(1)}, bf16[2,192,1152]{2,1,0:T(8,128)(2,1)}, u32[]{:S(2)}) copy-start(bf16[2,192,1152]{2,1,0:T(8,128)(2,1)} %param.19) | copy-start | bytes 2654212
  936.7 168.7 %copy-start.66 = (f32[1152]{0:T(1024)S(1)}, f32[1152]{0:T(1024)}, u32[]{:S(2)}) copy-start(f32[1152]{0:T(1024)} %copy-done.65) | copy-start | bytes 13828
  936.7 168.7 %copy-start.77 = (f32[192]{0:T(256)S(1)}, f32[192]{0:T(256)}, u32[]{:S(2)}) copy-start(f32[192]{0:T(256)} %copy-done.76) | copy-start | bytes 2308
  936.7 168.7 %copy-start.79 = (f32[192]{0:T(256)S(1)}, f32[192]{0:T(256)}, u32[]{:S(2)}) copy-start(f32[192]{0:T(256)} %copy-done.78) | copy-start | bytes 2308
  936.7 168.7 %copy-start.83 = (f32[192]{0:T(256)S(1)}, f32[192]{0:T(256)}, u32[]{:S(2)}) copy-start(f32[192]{0:T(256)} %copy-done.82) | copy-start | bytes 2308
  936.7 168.7 %copy-start.85 = (f32[192]{0:T(256)S(1)}, f32[192]{0:T(256)}, u32[]{:S(2)}) copy-start(f32[192]{0:T(256)} %copy-done.84) | copy-start | bytes 2308
  940.4 208.6 %copy-start.14 = (f32[192,1152]{1,0:T(8,128)S(1)}, f32[192,1152]{1,0:T(8,128)}, u32[]{:S(2)}) copy-start(f32[192,1152]{1,0:T(8,128)} %copy-done.13) | copy-start | bytes 2654212
  940.4 208.6 %copy-start.15 = (f32[192,1152]{1,0:T(8,128)S(1)}, f32[192,1152]{1,0:T(8,128)}, u32[]{:S(2)}) copy-start(f32[192,1152]{1,0:T(8,128)} %get-tuple-element.523) | copy-start | bytes 2654212
  (80 other events, 177.4 us)
Sparse Core Ops, SparseCore 0:
  16.6 44.1 all-gather.13
  63.1 40.2 all-gather.21
  135.5 75.9 reduce-scatter.16
  213.7 75.6 reduce-scatter.20
  743.7 39.9 all-gather.25
  785.8 40.2 all-gather.27
Sparse Core Ops, SparseCore 1:
  157.8 28.7 all-gather.17
  293.8 39.8 all-gather.23
  335.3 28.8 all-gather.19
  366.4 41.3 all-gather.31
  410.0 40.2 all-gather.15
  452.4 40.2 all-gather.29
  494.8 75.9 reduce-scatter.28
  573.0 75.5 reduce-scatter.24
  650.7 42.1 reduce-scatter.18
  695.2 42.1 reduce-scatter.22
  880.2 27.5 reduce-scatter.38
  910.9 37.2 reduce-scatter.36
  950.3 77.0 reduce-scatter.26
  1029.7 75.5 reduce-scatter.30
  1109.0 41.5 reduce-scatter.32
  1154.1 42.0 reduce-scatter.34
where the time goes:
time: 1210 us; the launch traced here: 1200 us
  waiting for transfers between devices  795 us (66%)
  matrix products  193 us (16%)
  local copies, waits for them, and re-layouts  72.1 us (6%)
  blocking collectives  72 us (6%)
  other arithmetic  50.9 us (4%)
  between operations  17.4 us (1%)
    reduce_scatter x2, waiting for transfers between devices, on_device(): lax.psum_scatter(jnp.einsum('krx,kdx->rd', triple_half, in_whole, preferr...  152 us
    reduce_scatter x2, waiting for transfers between devices, on_device(): lax.psum_scatter(product(context, out_whole), 'tensor', scatter_dimension...  133 us
    reduce_scatter x2, waiting for transfers between devices, on_device(): lax.psum_scatter(product_right_t(pre_half, up_whole), 'tensor', scatter_d...  124 us
    reduce_scatter x2, waiting for transfers between devices, on_device(): lax.psum_scatter(product(hidden, down_whole).astype(jnp.bfloat16), 'tenso...  83.8 us
    all_gather x2, waiting for transfers between devices, on_device(): grad_full = lax.all_gather(grad_rows, 'tensor', axis=0, tiled=True)  79.5 us
    all_gather x2, waiting for transfers between devices, on_device(): second_full = lax.all_gather(second_norm, 'tensor', axis=0, tiled=True)  61.6 us
    reduce_scatter x1, waiting for transfers between devices, on_device(): lax.psum_scatter(down_sum, 'fsdp', scatter_dimension=1, tiled=True)  43.9 us
    all_gather x2, waiting for transfers between devices, on_device(): first_full = lax.all_gather(first_norm, 'tensor', axis=0, tiled=True)  43.3 us
  transfers between devices with their start and end apart: 22, of which 18 were waited for; matrix products, arithmetic and copies ran while one was open for 18% of the time, Pallas kernels for 0%

commit v1 on v0

v1 whole, which is shorter than its diff:
```python
import functools
import math

import jax
import jax.numpy as jnp
from jax import lax
from jax.experimental import pallas as pl
from jax.experimental.pallas import tpu as pltpu
from jax.sharding import Mesh
from jax.sharding import PartitionSpec as P

DH = 72
IMG = 729
IMG_MB = 2
EPS = 1e-06
GELU_C = 0.7978845608028654
F32 = jnp.float32
BF16 = jnp.bfloat16
FSDP = ("fy", "fx")
SCALE = DH ** (-0.5)
LOG2E = math.log2(math.e)


def norm_forward(values, norm_gain, norm_shift):
    center = values - jnp.mean(values, axis=-1, keepdims=True)
    factor = lax.rsqrt(jnp.mean(center * center, axis=-1, keepdims=True) + EPS)
    scaled = center * factor
    return (scaled * norm_gain + norm_shift, scaled, factor)


def norm_backward(upstream, scaled, factor, norm_gain):
    inside = upstream * norm_gain
    return factor * (
        inside
        - jnp.mean(inside, axis=-1, keepdims=True)
        - scaled * jnp.mean(inside * scaled, axis=-1, keepdims=True)
    )


def gelu(pre_act):
    return (
        0.5
        * pre_act
        * (1.0 + jnp.tanh(GELU_C * (pre_act + 0.044715 * pre_act * pre_act * pre_act)))
    )


def gelu_back(pre_act, upstream):
    return jax.vjp(gelu, pre_act)[1](upstream)[0]


def dot_nn(left, right):
    return lax.dot_general(left, right, (((1,), (0,)), ((), ())), preferred_element_type=F32)


def dot_nt(left, right):
    return lax.dot_general(left, right, (((1,), (1,)), ((), ())), preferred_element_type=F32)


def dot_tn(left, right):
    return lax.dot_general(left, right, (((0,), (0,)), ((), ())), preferred_element_type=F32)


def sum_products(lefts, rights):
    total = dot_nt(lefts[0], rights[0])
    for left, right in zip(lefts[1:], rights[1:]):
        total = total + dot_nt(left, right)
    return total


def round_up(value, unit):
    return -(-value // unit) * unit


def swap(value, axis):
    return lax.ppermute(value, axis, [(0, 1), (1, 0)])


def slot_swap(value, stride, slots):
    return lax.ppermute(value, "slot", [(s, s ^ stride) for s in range(slots)])


def part_sum(value, parts):
    value = value.astype(BF16)
    if parts == 2:
        return value.astype(F32) + swap(value, "part").astype(F32)
    return lax.psum(value.astype(F32), "part")


def part_gather(value, parts):
    if parts == 2:
        other = swap(value, "part")
        first = lax.axis_index("part") == 0
        return jnp.stack([jnp.where(first, value, other), jnp.where(first, other, value)])
    return lax.all_gather(value, "part", axis=0)


def add_half(left, right):
    return (left.astype(F32) + right.astype(F32)).astype(BF16)


MESH = pl.DeviceIdType.MESH


class Place:
    def __init__(self):
        self.y, self.x = lax.axis_index("fy"), lax.axis_index("fx")
        self.z = lax.axis_index("slot")
        self.f = 2 * self.y + self.x
        self.across_x, self.across_y = {"fx": 1 - self.x}, {"fy": 1 - self.y}
        self.above = {"slot": jnp.minimum(self.z + 1, 3)}
        self.below = {"slot": jnp.maximum(self.z - 1, 0)}

    def barrier(self):
        z, sem = self.z, pltpu.get_barrier_semaphore()
        signal = lambda device: pl.semaphore_signal(sem, inc=1, device_id=device, device_id_type=MESH)
        signal(self.across_x)
        signal(self.across_y)

        @pl.when(z < 3)
        def _():
            signal(self.above)

        @pl.when(z > 0)
        def _():
            signal(self.below)

        pl.semaphore_wait(sem, 2 + jnp.where(z < 3, 1, 0) + jnp.where(z > 0, 1, 0))

    def far_first(self, i):
        low = self.z < 2
        near = jnp.where(low, self.z, 3 - self.z)
        at = jnp.where(i == 0, 3, jnp.where(i == 1, 2, jnp.where(i == 2, 1 - near, near)))
        return jnp.where(low, at, 3 - at)


def send(src, dst, send_sem, recv_sem, device):
    return pltpu.make_async_remote_copy(
        src_ref=src, dst_ref=dst, send_sem=send_sem, recv_sem=recv_sem, device_id=device, device_id_type=MESH
    )


class Gather:
    SEMS = 11

    def __init__(self, place, shards, w, sems, local_sem, rows):
        self.p, self.shards, self.w, self.rows = place, shards, w, rows
        (self.zr, self.zu, self.zd, self.xr, self.xs, self.yr, self.ys, self.ar, self.asn, self.br, self.bs) = sems
        self.local_sem = local_sem

    def block(self, k, slot, owner, half=None):
        at, count = owner * self.rows, self.rows
        if half is not None:
            count = count // 2
            at = at + half * count
        return self.w[k].at[slot, pl.ds(pl.multiple_of(at, 16), count), :]

    def mine(self, k, slot, shard):
        return self.shards[k] if shard else self.block(k, slot, self.p.f)

    def up(self, k, slot, shard=False):
        dst = self.block(k, slot, self.p.f)
        return send(self.mine(k, slot, shard), dst, self.zu.at[k, slot], self.zr.at[k, slot], self.p.above)

    def down(self, k, slot, shard=False):
        dst = self.block(k, slot, self.p.f)
        return send(self.mine(k, slot, shard), dst, self.zd.at[k, slot], self.zr.at[k, slot], self.p.below)

    def to_x(self, k, slot, shard=False):
        dst = self.block(k, slot, self.p.f)
        return send(self.mine(k, slot, shard), dst, self.xs.at[k, slot], self.xr.at[k, slot], self.p.across_x)

    def to_y(self, k, slot, shard=False):
        dst = self.block(k, slot, self.p.f)
        return send(self.mine(k, slot, shard), dst, self.ys.at[k, slot], self.yr.at[k, slot], self.p.across_y)

    def from_x(self, k, slot):
        ref = self.block(k, slot, self.p.f ^ 1)
        return send(ref, ref, self.xs.at[k, slot], self.xr.at[k, slot], self.p.across_x)

    def from_y(self, k, slot):
        ref = self.block(k, slot, self.p.f ^ 2)
        return send(ref, ref, self.ys.at[k, slot], self.yr.at[k, slot], self.p.across_y)

    def corner_y(self, k, slot):
        ref = self.block(k, slot, self.p.f ^ 1, 0)
        return send(ref, ref, self.asn.at[k, slot], self.ar.at[k, slot], self.p.across_y)

    def corner_x(self, k, slot):
        ref = self.block(k, slot, self.p.f ^ 2, 1)
        return send(ref, ref, self.bs.at[k, slot], self.br.at[k, slot], self.p.across_x)

    def wait_corner(self, k, slot):
        ref = self.block(k, slot, self.p.f ^ 3, 0)
        send(ref, ref, self.asn.at[k, slot], self.ar.at[k, slot], self.p.across_y).wait_recv()
        ref = self.block(k, slot, self.p.f ^ 3, 1)
        send(ref, ref, self.bs.at[k, slot], self.br.at[k, slot], self.p.across_x).wait_recv()

    def local(self, k):
        return pltpu.make_async_copy(self.shards[k], self.block(k, self.p.z, self.p.f), self.local_sem.at[k])

    def start_z(self, k):
        @pl.when(self.p.z < 3)
        def _():
            self.up(k, self.p.z, True).start()

        @pl.when(self.p.z > 0)
        def _():
            self.down(k, self.p.z, True).start()

    def start_xy(self, k):
        self.to_x(k, self.p.z, True).start()
        self.to_y(k, self.p.z, True).start()
        self.local(k).start()

    def pass_on(self, k, d):
        z = self.p.z

        @pl.when(z >= d)
        def _():
            self.up(k, z - d).wait_recv()

            @pl.when(z < 3)
            def _():
                self.up(k, z - d).start()

            self.to_x(k, z - d).start()
            self.to_y(k, z - d).start()

        @pl.when(z + d <= 3)
        def _():
            self.down(k, z + d).wait_recv()

            @pl.when(z > 0)
            def _():
                self.down(k, z + d).start()

            self.to_x(k, z + d).start()
            self.to_y(k, z + d).start()

    def corner(self, k, d):
        def one(slot):
            self.from_x(k, slot).wait_recv()
            self.corner_y(k, slot).start()
            self.from_y(k, slot).wait_recv()
            self.corner_x(k, slot).start()

        z = self.p.z
        if d == 0:
            one(z)
        else:
            pl.when(z >= d)(lambda: one(z - d))
            pl.when(z + d <= 3)(lambda: one(z + d))

    def arrive(self, k):
        self.local(k).wait()
        for slot in range(4):
            self.wait_corner(k, slot)

    def drain(self, k):
        z = self.p.z
        for slot in range(4):
            self.to_x(k, slot).wait_send()
            self.to_y(k, slot).wait_send()
            self.corner_y(k, slot).wait_send()
            self.corner_x(k, slot).wait_send()

            @pl.when((z < 3) & (slot <= z))
            def _(slot=slot):
                self.up(k, slot).wait_send()

            @pl.when((z > 0) & (slot >= z))
            def _(slot=slot):
                self.down(k, slot).wait_send()


def gather_kernel(*refs, count, rows):
    shards, w = refs[:count], refs[count : 2 * count]
    sems = refs[2 * count :]
    place = Place()
    place.barrier()
    g = Gather(place, shards, w, sems[:-1], sems[-1], rows)
    g.start_z(0)
    for k in range(count):
        g.start_xy(k)
        g.pass_on(k, 1)
        g.corner(k, 0)
        g.pass_on(k, 2)
        g.corner(k, 1)
        g.pass_on(k, 3)
        if k + 1 < count:
            g.start_z(k + 1)
        g.corner(k, 2)
        g.corner(k, 3)
    for k in range(count):
        g.arrive(k)
        g.drain(k)


def gather_weights(shards, paired):
    if not paired:
        slots = lax.axis_size("slot")
        whole = [lax.all_gather(s, ("slot",) + FSDP, axis=0) for s in shards]
        return [w.reshape(slots, -1, w.shape[-1]) for w in whole]
    count, rows = len(shards), shards[0].shape[0]
    return pl.pallas_call(
        functools.partial(gather_kernel, count=count, rows=rows),
        in_specs=[pl.BlockSpec(memory_space=pltpu.VMEM)] * count,
        out_specs=[pl.BlockSpec(memory_space=pl.ANY)] * count,
        out_shape=[jax.ShapeDtypeStruct((4, 4 * rows, s.shape[1]), BF16) for s in shards],
        scratch_shapes=[pltpu.SemaphoreType.DMA((count, 4))] * Gather.SEMS + [pltpu.SemaphoreType.DMA((count,))],
        compiler_params=pltpu.CompilerParams(collective_id=1, has_side_effects=True),
        name="gather",
    )(*shards)


class Reduce:
    SEMS = 16

    def __init__(self, place, g, out, bufs, sems, rows):
        self.p, self.g, self.out, self.rows = place, g, out, rows
        self.bufs, self.sems = bufs, sems

    def grad(self, k, slot, owner, half=None):
        at, count = owner * self.rows, self.rows
        if half is not None:
            count = count // 2
            at = at + half * count
        return self.g[k].at[slot, pl.ds(pl.multiple_of(at, 16), count), :]

    def half(self, ref, slot, half):
        count = self.rows // 2
        return ref.at[slot, half * count : (half + 1) * count, :]

    def copy(self, k, slot, src, dst, index, device):
        return send(src, dst, self.sems[2 * index].at[k, slot], self.sems[2 * index + 1].at[k, slot], device)

    def corner_y(self, k, s):
        return self.copy(k, s, self.grad(k, s, self.p.f ^ 3, 0), self.bufs[k][0].at[s], 0, self.p.across_y)

    def corner_x(self, k, s):
        return self.copy(k, s, self.grad(k, s, self.p.f ^ 3, 1), self.bufs[k][1].at[s], 1, self.p.across_x)

    def x_low(self, k, s):
        return self.copy(k, s, self.bufs[k][0].at[s], self.half(self.bufs[k][2], s, 0), 2, self.p.across_x)

    def x_high(self, k, s):
        dst = self.half(self.bufs[k][2], s, 1)
        return self.copy(k, s, self.grad(k, s, self.p.f ^ 1, 1), dst, 3, self.p.across_x)

    def y_low(self, k, s):
        dst = self.half(self.bufs[k][3], s, 0)
        return self.copy(k, s, self.grad(k, s, self.p.f ^ 2, 0), dst, 4, self.p.across_y)

    def y_high(self, k, s):
        return self.copy(k, s, self.bufs[k][1].at[s], self.half(self.bufs[k][3], s, 1), 5, self.p.across_y)

    def up(self, k, s):
        return self.copy(k, s, self.bufs[k][2].at[s], self.bufs[k][4].at[s], 6, self.p.above)

    def down(self, k, s):
        return self.copy(k, s, self.bufs[k][2].at[s], self.bufs[k][5].at[s], 7, self.p.below)

    def start(self, k):
        def one(i, carry):
            s = self.p.far_first(i)
            self.corner_y(k, s).start()
            self.corner_x(k, s).start()
            self.y_low(k, s).start()
            self.x_high(k, s).start()
            return carry

        lax.fori_loop(0, 4, one, 0)

    def tiles(self, rows, body):
        step = 48 if rows % 48 == 0 else 16

        def one(t, carry):
            body(pl.ds(pl.multiple_of(t * step, 16), step))
            return carry

        lax.fori_loop(0, rows // step, one, 0)

    def middle(self, k):
        count = self.rows // 2

        def one(i, carry):
            s = self.p.far_first(i)
            low, high = self.bufs[k][0], self.bufs[k][1]
            self.corner_y(k, s).wait_recv()
            own = self.grad(k, s, self.p.f ^ 1, 0)

            def add_low(span):
                low[s, span, :] = add_half(low[s, span, :], own[span, :])

            self.tiles(count, add_low)
            self.x_low(k, s).start()
            self.corner_x(k, s).wait_recv()
            other = self.grad(k, s, self.p.f ^ 2, 1)

            def add_high(span):
                high[s, span, :] = add_half(high[s, span, :], other[span, :])

            self.tiles(count, add_high)
            self.y_high(k, s).start()
            return carry

        lax.fori_loop(0, 4, one, 0)

    def line(self, k):
        z, acc, side = self.p.z, self.bufs[k][2], self.bufs[k][3]
        lower, upper = self.bufs[k][4], self.bufs[k][5]

        def one(i, carry):
            s = self.p.far_first(i)
            self.x_low(k, s).wait_recv()
            self.x_high(k, s).wait_recv()
            self.y_low(k, s).wait_recv()
            self.y_high(k, s).wait_recv()
            own = self.grad(k, s, self.p.f)

            def add(span):
                total = own[span, :].astype(F32) + acc[s, span, :].astype(F32) + side[s, span, :].astype(F32)
                acc[s, span, :] = total.astype(BF16)

            def add_from(ref):
                def body(span):
                    acc[s, span, :] = add_half(acc[s, span, :], ref[s, span, :])

                return body

            self.tiles(self.rows, add)

            @pl.when((z > 0) & (s >= z))
            def _():
                self.up(k, s).wait_recv()
                self.tiles(self.rows, add_from(lower))

            @pl.when((z < 3) & (s <= z))
            def _():
                self.down(k, s).wait_recv()
                self.tiles(self.rows, add_from(upper))

            @pl.when(s > z)
            def _():
                self.up(k, s).start()

            @pl.when(s < z)
            def _():
                self.down(k, s).start()

            @pl.when(s == z)
            def _():
                def final(span):
                    self.out[k][span, :] = acc[s, span, :].astype(F32)

                self.tiles(self.rows, final)

            return carry

        lax.fori_loop(0, 4, one, 0)

    def drain(self, k):
        def one(s, carry):
            for copy in (self.corner_y, self.corner_x, self.x_low, self.x_high, self.y_low, self.y_high):
                copy(k, s).wait_send()

            @pl.when(s > self.p.z)
            def _():
                self.up(k, s).wait_send()

            @pl.when(s < self.p.z)
            def _():
                self.down(k, s).wait_send()

            return carry

        lax.fori_loop(0, 4, one, 0)


def reduce_buffers(rows, lanes):
    return [
        pltpu.VMEM((4, rows // 2, lanes), BF16),
        pltpu.VMEM((4, rows // 2, lanes), BF16),
        pltpu.VMEM((4, rows, lanes), BF16),
        pltpu.VMEM((4, rows, lanes), BF16),
        pltpu.VMEM((4, rows, lanes), BF16),
        pltpu.VMEM((4, rows, lanes), BF16),
    ]


def reduce_kernel(*refs, count, rows):
    g, out = refs[:count], refs[count : 2 * count]
    bufs = [refs[2 * count + 6 * k : 2 * count + 6 * k + 6] for k in range(count)]
    sems = refs[8 * count :]
    place = Place()
    place.barrier()
    r = Reduce(place, g, out, bufs, sems, rows)
    r.start(0)
    for k in range(count):
        r.middle(k)
        if k + 1 < count:
            r.start(k + 1)
        r.line(k)
    for k in range(count):
        r.drain(k)


def scatter_grads(chunks, paired):
    if not paired:
        count = lax.axis_size("fy") * lax.axis_size("fx")
        split = [c.reshape(c.shape[0] * count, c.shape[1] // count, c.shape[2]) for c in chunks]
        return [lax.psum_scatter(c, ("slot",) + FSDP, scatter_dimension=0).astype(F32) for c in split]
    count, rows = len(chunks), chunks[0].shape[1] // 4
    scratch = [b for c in chunks for b in reduce_buffers(rows, c.shape[2])]
    return pl.pallas_call(
        functools.partial(reduce_kernel, count=count, rows=rows),
        in_specs=[pl.BlockSpec(memory_space=pltpu.VMEM)] * count,
        out_specs=[pl.BlockSpec(memory_space=pltpu.VMEM)] * count,
        out_shape=[jax.ShapeDtypeStruct((rows, c.shape[2]), F32) for c in chunks],
        scratch_shapes=scratch + [pltpu.SemaphoreType.DMA((count, 4))] * Reduce.SEMS,
        compiler_params=pltpu.CompilerParams(
            collective_id=2, has_side_effects=True, vmem_limit_bytes=64000000
        ),
        name="reduce",
    )(*chunks)


def attend_kernel(x_ref, w_ref, b_ref, segc_ref, segr_ref, qkv_ref, ctx_ref, inv_ref, part_ref, *, cols, tile):
    rows = x_ref.shape[0]
    heads = cols // DH
    block = pl.program_id(0)
    projected = dot_nn(x_ref[...], w_ref[0, :, : 3 * cols]) + b_ref[0]
    qkv_ref[0] = projected.astype(BF16)
    for head in range(heads):
        lo = head * DH
        keys = qkv_ref[0, :, cols + lo : cols + lo + DH]
        values = qkv_ref[0, :, 2 * cols + lo : 2 * cols + lo + DH]

        def one_tile(t, carry):
            span = pl.ds(pl.multiple_of(t * tile, tile), tile)
            scores = dot_nt(qkv_ref[0, span, lo : lo + DH], keys)
            allowed = segc_ref[span, :] == segr_ref[...]
            exact = jnp.where(allowed, jnp.exp2(scores * (SCALE * LOG2E)), 0.0)
            inverse = 1.0 / jnp.sum(exact, axis=1, keepdims=True)
            context = dot_nn(exact.astype(BF16), values) * inverse
            ctx_ref[0, span, lo : lo + DH] = context.astype(BF16)
            inv_ref[0, span, head : head + 1] = inverse
            return carry

        lax.fori_loop(0, rows // tile, one_tile, 0)
    part = dot_nt(ctx_ref[0], w_ref[0, :, 3 * cols : 4 * cols])

    @pl.when(block == 0)
    def _():
        part_ref[...] = part

    @pl.when(block > 0)
    def _():
        part_ref[...] += part


def attend(first_norm, weights, bias, segments, cols, tile):
    rows, width = first_norm.shape
    slots, _, lanes = weights.shape
    heads = cols // DH
    whole = lambda shape: pl.BlockSpec(shape, lambda s: (0,) * len(shape))
    each = lambda shape: pl.BlockSpec((1,) + shape, lambda s: (s, 0, 0))
    return pl.pallas_call(
        functools.partial(attend_kernel, cols=cols, tile=tile),
        grid=(slots,),
        in_specs=[
            whole((rows, width)),
            each((width, lanes)),
            each((1, 3 * cols)),
            whole((rows, 1)),
            whole((1, rows)),
        ],
        out_specs=[each((rows, 3 * cols)), each((rows, cols)), each((rows, heads)), whole((rows, width))],
        out_shape=[
            jax.ShapeDtypeStruct((slots, rows, 3 * cols), BF16),
            jax.ShapeDtypeStruct((slots, rows, cols), BF16),
            jax.ShapeDtypeStruct((slots, rows, heads), F32),
            jax.ShapeDtypeStruct((rows, width), F32),
        ],
        cost_estimate=pl.CostEstimate(
            flops=slots * (8 * rows * width * cols + 4 * rows * rows * 256 * heads),
            bytes_accessed=slots * width * lanes * 2 + rows * width * 10,
            transcendentals=slots * heads * rows * rows,
        ),
        name="attend",
    )(first_norm, weights, bias, segments[:, None], segments[None, :])


def attend_back_kernel(
    r_ref, w_ref, qkv_ref, ctx_ref, inv_ref, segc_ref, segr_ref, grad_ref, bias_ref, back_ref, key_acc, value_acc, *, cols, tile
):
    rows = r_ref.shape[0]
    heads = cols // DH
    back_ref[...] = dot_nn(r_ref[...], w_ref[0, :, 3 * cols : 4 * cols]).astype(BF16)
    ones = jnp.ones((8, DH), F32)
    for head in range(heads):
        lo = head * DH
        keys = qkv_ref[0, :, cols + lo : cols + lo + DH]
        values = qkv_ref[0, :, 2 * cols + lo : 2 * cols + lo + DH]
        key_acc[...] = jnp.zeros_like(key_acc)
        value_acc[...] = jnp.zeros_like(value_acc)

        def one_tile(t, query_total):
            span = slice(t * tile, (t + 1) * tile)
            queries = qkv_ref[0, span, lo : lo + DH]
            back = (back_ref[span, lo : lo + DH].astype(F32) * inv_ref[0, span, head : head + 1]).astype(BF16)
            along = back.astype(F32) * ctx_ref[0, span, lo : lo + DH].astype(F32)
            delta = lax.dot_general(
                ones, along, (((1,), (1,)), ((), ())), precision=lax.Precision.HIGHEST, preferred_element_type=F32
            )[:1]
            scores = dot_nt(keys, queries)
            allowed = segc_ref[...] == segr_ref[:, span]
            exact = jnp.where(allowed, jnp.exp2(scores * (SCALE * LOG2E)), 0.0)
            value_acc[...] += dot_nn(exact.astype(BF16), back)
            prob_grad = dot_nt(values, back)
            score_grad = (exact * (prob_grad - delta)).astype(BF16)
            key_acc[...] += dot_nn(score_grad, queries)
            query_grad = dot_tn(score_grad, keys) * SCALE
            grad_ref[0, span, lo : lo + DH] = query_grad.astype(BF16)
            return query_total + jnp.sum(query_grad, axis=0, keepdims=True)

        tiles = rows // tile
        query_total = jnp.zeros((1, DH), F32)
        for t in range(tiles):
            query_total = one_tile(t, query_total)
        grad_ref[0, :, cols + lo : cols + lo + DH] = (key_acc[...] * SCALE).astype(BF16)
        grad_ref[0, :, 2 * cols + lo : 2 * cols + lo + DH] = value_acc[...].astype(BF16)
        bias_ref[0, 0:1, lo : lo + DH] = query_total
        bias_ref[0, 1:2, lo : lo + DH] = jnp.sum(value_acc[...], axis=0, keepdims=True)


def attend_back(residual_half, weights, qkv, context, inverse, segments, cols, tile):
    rows, width = residual_half.shape
    slots, _, lanes = weights.shape
    heads = cols // DH
    whole = lambda shape: pl.BlockSpec(shape, lambda s: (0,) * len(shape))
    each = lambda shape: pl.BlockSpec((1,) + shape, lambda s: (s, 0, 0))
    return pl.pallas_call(
        functools.partial(attend_back_kernel, cols=cols, tile=tile),
        grid=(slots,),
        in_specs=[
            whole((rows, width)),
            each((width, lanes)),
            each((rows, 3 * cols)),
            each((rows, cols)),
            each((rows, heads)),
            whole((rows, 1)),
            whole((1, rows)),
        ],
        out_specs=[each((rows, 3 * cols)), each((2, cols))],
        out_shape=[
            jax.ShapeDtypeStruct((slots, rows, 3 * cols), BF16),
            jax.ShapeDtypeStruct((slots, 2, cols), F32),
        ],
        scratch_shapes=[
            pltpu.VMEM((rows, cols), BF16),
            pltpu.VMEM((rows, DH), F32),
            pltpu.VMEM((rows, DH), F32),
        ],
        cost_estimate=pl.CostEstimate(
            flops=slots * (2 * rows * width * cols + 10 * rows * rows * 256 * heads),
            bytes_accessed=slots * width * lanes * 2 + rows * width * 10,
            transcendentals=slots * heads * rows * rows,
        ),
        name="attend_back",
    )(residual_half, weights, qkv, context, inverse, segments[:, None], segments[None, :])


def on_device(
    block_input,
    segment_ids,
    norm_gains,
    row_biases,
    in_projection,
    query_value_bias,
    out_projection,
    up_weight,
    unit_bias,
    down_weight,
    cotangent,
):
    local, rows_each, width = block_input.shape
    rows_mb = segment_ids.shape[1]
    cols = in_projection.shape[2]
    units = up_weight.shape[1]
    shard_rows = up_weight.shape[0]
    slots, parts = lax.axis_size("slot"), lax.axis_size("part")
    paired = lax.axis_size("fy") == 2 and lax.axis_size("fx") == 2 and slots == 4 and shard_rows % 32 == 0
    slot, part = lax.axis_index("slot"), lax.axis_index("part")
    fsdp_index = lax.axis_index("fy") * lax.axis_size("fx") + lax.axis_index("fx")
    batch, image = slot % local, slot // local
    late = image == 1

    half_rows = rows_mb // IMG_MB
    padding = rows_mb - IMG_MB * IMG
    edge = round_up(max(half_rows - IMG, padding - (half_rows - IMG)), 16)
    tail = round_up(padding, 16)
    rows = round_up(half_rows + edge + tail, 128)
    filler = rows - half_rows - edge - tail

    def edges(main):
        near = jnp.where(late, main[:edge], main[half_rows - edge :])
        far = main[half_rows - tail :]
        return jnp.concatenate([near, far])

    def to_slot(value):
        mine = lax.dynamic_index_in_dim(value, batch, 0, keepdims=False)
        send = lax.dynamic_index_in_dim(value, 1 - batch, 0, keepdims=False)
        other = slot_swap(send, 1, slots)
        pair = jnp.where(batch == 0, jnp.stack([mine, other]), jnp.stack([other, mine]))
        main = part_gather(pair, parts).swapaxes(0, 1).reshape(half_rows, width)
        beyond = slot_swap(edges(main), local, slots)
        return jnp.concatenate([main, beyond, jnp.zeros((filler, width), value.dtype)])

    def from_slot(value, owned):
        main = value[:half_rows]
        beyond = slot_swap(value[half_rows : half_rows + edge + tail], local, slots)
        keep = owned[:half_rows, None]
        near, far = beyond[:edge], beyond[edge:]
        blank = lambda count: jnp.zeros((count, width), value.dtype)
        early_fill = jnp.concatenate([blank(half_rows - edge), near])
        late_fill = jnp.concatenate([near, blank(half_rows - edge - tail), far])
        main = jnp.where(keep, main, jnp.where(late, late_fill, early_fill))
        main = main.reshape(local, parts, rows_each, width)
        mine = lax.dynamic_index_in_dim(main, part, 1, keepdims=False)
        stay = lax.dynamic_index_in_dim(mine, batch, 0, keepdims=False)
        other = slot_swap(lax.dynamic_index_in_dim(mine, 1 - batch, 0, keepdims=False), 1, slots)
        return jnp.where(batch == 0, jnp.stack([stay, other]), jnp.stack([other, stay]))

    ids = lax.dynamic_index_in_dim(segment_ids, batch, 0, keepdims=False)
    fill_ids = jnp.full((filler,), -2, jnp.int32)
    early_ids = jnp.concatenate([ids[: half_rows + edge], ids[rows_mb - tail :], fill_ids])
    late_ids = jnp.concatenate(
        [ids[half_rows:], ids[half_rows - edge : half_rows], jnp.full((tail,), -2, jnp.int32), fill_ids]
    )
    segments = jnp.where(late, late_ids, early_ids)
    image_id = (fsdp_index * local + batch) * IMG_MB + image
    owned = (segments == image_id) | (jnp.logical_not(late) & (segments == -1))

    main_units = units // 128 * 128
    rest = units - main_units
    in_lanes = 3 * cols
    small = in_lanes + cols + 2 * rest
    high = query_value_bias.astype(BF16)
    low = (query_value_bias - high.astype(F32)).astype(BF16)
    vectors = jnp.concatenate([high.reshape(-1), low.reshape(-1), unit_bias])
    extra = -(-vectors.shape[0] // shard_rows)
    lanes = round_up(small + extra, 128)
    vectors = jnp.pad(vectors, (0, extra * shard_rows - vectors.shape[0])).reshape(shard_rows, extra)
    down_t = down_weight.T
    small_shard = jnp.concatenate(
        [
            in_projection.transpose(1, 0, 2).reshape(shard_rows, in_lanes),
            out_projection.T,
            up_weight[:, main_units:],
            down_t[:, main_units:],
            vectors,
            jnp.zeros((shard_rows, lanes - small - extra), BF16),
        ],
        axis=1,
    )
    small_all, up_main, down_main = gather_weights(
        [small_shard, up_weight[:, :main_units], down_t[:, :main_units]], paired
    )
    small_blocks, up_blocks, down_blocks = list(small_all), list(up_main), list(down_main)
    vectors = jnp.stack([b[:shard_rows, small : small + extra].reshape(-1) for b in small_blocks])
    qv_all = vectors[:, : 2 * cols].astype(F32) + vectors[:, 2 * cols : 4 * cols].astype(F32)
    unit_all = vectors[:, 4 * cols : 4 * cols + units].astype(F32)

    bias = jnp.concatenate([qv_all[:, :cols], jnp.zeros((slots, cols), F32), qv_all[:, cols:]], axis=1)[:, None]
    rest_lanes = round_up(slots * rest, 128)
    rest_pad = rest_lanes - slots * rest

    def unit_layout(blocks, at):
        extra = [b[:, at : at + rest] for b in small_blocks]
        return blocks + [jnp.concatenate(extra + [jnp.zeros((width, rest_pad), BF16)], axis=1)]

    gains, shifts = norm_gains, row_biases

    x_float = to_slot(block_input).astype(F32)
    grad_rows = jnp.where(owned[:, None], to_slot(cotangent), 0)
    upstream = grad_rows.astype(F32)

    first_out, first_scaled, first_factor = norm_forward(x_float, gains[0], shifts[0])
    first_norm = first_out.astype(BF16)
    qkv, context, inverse, attention_part = attend(
        first_norm, small_all, bias, segments, cols, rows // 2
    )
    residual = x_float + part_sum(attention_part, parts) + shifts[2]
    second_out, second_scaled, second_factor = norm_forward(residual, gains[1], shifts[1])
    second_norm = second_out.astype(BF16)
    up_all = unit_layout(up_blocks, in_lanes + cols)
    down_all = unit_layout(down_blocks, in_lanes + cols + rest)
    unit_rows = [unit_all[s, :main_units] for s in range(slots)]
    unit_rows += [jnp.concatenate([unit_all[:, main_units:].reshape(-1), jnp.zeros((rest_pad,), F32)])]
    pre_acts = [dot_nn(second_norm, w) + b for w, b in zip(up_all, unit_rows)]
    hiddens = [gelu(p).astype(BF16) for p in pre_acts]
    unit_part = sum_products(hiddens, down_all)
    unit_part = part_sum(unit_part, parts)
    output = from_slot((residual + unit_part + shifts[3]).astype(BF16), owned)

    down_sums = [dot_tn(grad_rows, h).astype(BF16) for h in hiddens]
    pre_grads = [gelu_back(p, dot_nn(grad_rows, w)) for p, w in zip(pre_acts, down_all)]
    pre_halves = [p.astype(BF16) for p in pre_grads]
    unit_sums = [jnp.sum(p, axis=0) for p in pre_grads]
    up_sums = [dot_tn(second_norm, p).astype(BF16) for p in pre_halves]
    second_grad = part_sum(sum_products(pre_halves, up_all), parts)
    residual_grad = upstream + norm_backward(second_grad, second_scaled, second_factor, gains[1])
    residual_half = residual_grad.astype(BF16)
    out_sum = [dot_tn(residual_half, context[s]).astype(BF16) for s in range(slots)]
    triple, bias_sum = attend_back(
        residual_half, small_all, qkv, context, inverse, segments, cols, rows // 2
    )
    in_sum = [dot_tn(first_norm, triple[s]).astype(BF16) for s in range(slots)]
    first_part = sum_products([triple[s] for s in range(slots)], [b[:, :in_lanes] for b in small_blocks])
    first_grad = part_sum(first_part, parts)
    input_grad = residual_grad + norm_backward(first_grad, first_scaled, first_factor, gains[0])
    input_grad = from_slot(input_grad.astype(BF16), owned)

    rest_of = lambda sums, s: sums[slots][:, s * rest : (s + 1) * rest]
    blank = jnp.zeros((width, lanes - small), BF16)
    small_sums = [
        jnp.concatenate([in_sum[s], out_sum[s], rest_of(up_sums, s), rest_of(down_sums, s), blank], axis=1)
        for s in range(slots)
    ]
    down_grad, up_grad, small_grad = scatter_grads(
        [jnp.stack(down_sums[:slots]), jnp.stack(up_sums[:slots]), jnp.stack(small_sums)], paired
    )
    in_grad = small_grad[:, :in_lanes].reshape(shard_rows, 3, cols).transpose(1, 0, 2)
    out_grad = small_grad[:, in_lanes : in_lanes + cols].T
    at = in_lanes + cols
    up_grad = jnp.concatenate([up_grad, small_grad[:, at : at + rest]], axis=1)
    down_grad = jnp.concatenate([down_grad, small_grad[:, at + rest : at + 2 * rest]], axis=1).T

    rows_sum = jnp.stack(
        [
            jnp.sum(first_grad * first_scaled, axis=0),
            jnp.sum(second_grad * second_scaled, axis=0),
            jnp.sum(first_grad, axis=0),
            jnp.sum(second_grad, axis=0),
            jnp.sum(residual_grad, axis=0),
            jnp.sum(upstream, axis=0),
        ]
    )
    sums = [rows_sum, bias_sum] + unit_sums
    flat = jnp.concatenate([v.reshape(-1) for v in sums])
    total = jnp.pad(flat, (0, round_up(flat.shape[0], 1024) - flat.shape[0])).reshape(-1, 128)
    if paired:
        total = total + swap(total, "fx")
        total = total + swap(total, "fy")
        stride = 1
        while stride < slots:
            total = total + slot_swap(total, stride, slots)
            stride *= 2
    else:
        total = lax.psum(total, ("slot",) + FSDP)
    total = total.reshape(-1)
    parts_of, at = [], 0
    for v in sums:
        parts_of.append(total[at : at + v.size].reshape(v.shape))
        at += v.size
    rows_total, bias_total = parts_of[:2]
    bias_grad = lax.dynamic_index_in_dim(bias_total, slot, 0, keepdims=False)
    unit_grad = jnp.concatenate(
        [
            lax.dynamic_index_in_dim(jnp.stack(parts_of[2 : 2 + slots]), slot, 0, keepdims=False),
            lax.dynamic_slice_in_dim(parts_of[2 + slots], slot * rest, rest),
        ]
    )
    return (
        output,
        input_grad.astype(F32),
        rows_total[:2],
        rows_total[2:],
        in_grad,
        bias_grad,
        out_grad,
        up_grad,
        unit_grad,
        down_grad,
    )


def solution(mesh):
    fsdp, tensor = mesh.shape["fsdp"], mesh.shape["tensor"]

    def layer(*arrays):
        local = arrays[0].shape[0] // fsdp
        slots = local * IMG_MB
        assert local == 2 and slots == 4 and tensor % slots == 0 and fsdp % 2 == 0
        grid = Mesh(
            mesh.devices.reshape(fsdp // 2, 2, slots, tensor // slots), ("fy", "fx", "slot", "part")
        )
        tens = ("slot", "part")
        return jax.shard_map(
            on_device,
            mesh=grid,
            in_specs=(
                P(FSDP, tens, None),
                P(FSDP, None),
                P(),
                P(),
                P(None, FSDP, tens),
                P(None, tens),
                P(tens, FSDP),
                P(FSDP, tens),
                P(tens),
                P(tens, FSDP),
                P(FSDP, tens, None),
            ),
            out_specs=(
                P(FSDP, tens, None),
                P(FSDP, tens, None),
                P(),
                P(),
                P(None, FSDP, tens),
                P(None, tens),
                P(tens, FSDP),
                P(FSDP, tens),
                P(tens),
                P(tens, FSDP),
            ),
            check_vma=False,
        )(*arrays)

    return layer
```

time: 1210 us -> 646 us (0.53)
  waiting for transfers between devices: 795 us -> 47.9 us
  Pallas kernels: 0 us -> 366 us
  matrix products: 193 us -> 76.3 us
  blocking collectives: 72 us -> 0 us
  between operations: 17.4 us -> 2.41 us
    reduce_scatter x10 -> x0, waiting for transfers between devices: 537 us -> none  [the longest x2 152 us: on_device(): lax.psum_scatter(jnp.einsum('krx,kdx->rd', triple_half, in_whole, preferr...]
    pallas_call x0 -> x4, Pallas kernels: none -> 366 us  [the longest x1 152 us: scatter_grads(): pl.pallas_call(functools.partial(reduce_kernel, count=count, rows=rows),...]
    all_gather x10 -> x0, waiting for transfers between devices: 246 us -> none  [the longest x2 79.5 us: on_device(): grad_full = lax.all_gather(grad_rows, 'tensor', axis=0, tiled=True)]
    dot_general x50 -> x42, matrix products: 185 us -> 76.3 us  [the longest x18 31.6 us: dot_tn(): lax.dot_general(left, right, (((0,), (0,)), ((), ())), preferred_element_...]
    ppermute x0 -> x18, waiting for transfers between devices: none -> 47.9 us  [the longest x10 45.1 us: slot_swap(): return lax.ppermute(value, 'slot', [(s, s ^ stride) for s in range(slots)])]
    psum x1 -> x0, blocking collectives: 39.9 us -> none  [on_device(): lax.psum((gains_sum, shifts_sum, bias_wide, unit_wide), ('fsdp', 'tensor'))]
    all_gather x2 -> x0, blocking collectives: 32.1 us -> none  [the longest x1 20.9 us: fetch_forward(): lax.all_gather(in_projection, 'fsdp', axis=1, tiled=True)]
    unnamed x174 -> x156, local copies, waits for them, and re-layouts: 31.9 us -> 7.28 us
  transfers between devices with their start and end apart: 22 -> 18, of which waited for: 18 -> 7; matrix products, arithmetic and copies ran while one was open for 18% -> 20% of each run, Pallas kernels for 0% -> 50%
where the time goes in v1:
time: 646 us; the launch traced here: 640 us
  Pallas kernels  366 us (57%)
  matrix products  76.3 us (12%)
  local copies, waits for them, and re-layouts  76.1 us (12%)
  other arithmetic  59.4 us (9%)
  waiting for transfers between devices  47.9 us (7%)
  starting transfers between devices  12.1 us (2%)
    pallas_call x1, Pallas kernels, scatter_grads(): pl.pallas_call(functools.partial(reduce_kernel, count=count, rows=rows),...  152 us
    pallas_call x1, Pallas kernels, gather_weights(): pl.pallas_call(functools.partial(gather_kernel, count=count, rows=rows),...  140 us
    pallas_call x1, Pallas kernels, attend_back(): pl.pallas_call(functools.partial(attend_back_kernel, cols=cols, tile=tile...  45.8 us
    ppermute x10, waiting for transfers between devices, slot_swap(): return lax.ppermute(value, 'slot', [(s, s ^ stride) for s in range(slots)])  45.1 us
    dot_general x18, matrix products, dot_tn(): lax.dot_general(left, right, (((0,), (0,)), ((), ())), preferred_element_...  31.6 us
    pallas_call x1, Pallas kernels, attend(): pl.pallas_call(functools.partial(attend_kernel, cols=cols, tile=tile), gr...  27.8 us
    dot_general x14, matrix products, dot_nt(): lax.dot_general(left, right, (((1,), (1,)), ((), ())), preferred_element_...  23.7 us
    dot_general x10, matrix products, dot_nn(): lax.dot_general(left, right, (((1,), (0,)), ((), ())), preferred_element_...  21 us
  transfers between devices with their start and end apart: 18, of which 7 were waited for; matrix products, arithmetic and copies ran while one was open for 20% of the time, Pallas kernels for 50%

profile of v1, /device:TPU:0, one launch (start us, length us, event | category | flops | bytes accessed | tf_op | source)
XLA Modules:
  0.0 639.8 jit_solution(14508332734439474468)
XLA Ops:
  0.7 2.1 constant_dynamic-slice_fusion.3
  2.8 3.1 collective-permute-start.7
  12.2 140.4 %gather.1 = (bf16[4,1152,640]{2,1,0:T(8,128)(2,1)}, bf16[4,1152,512]{2,1,0:T(8,128)(2,1)}, bf16[4,1152,512]{2,1,0:T(8,128)(2,1)}) custom-call(bf16[288,640]{1,0:T(8,128)(2,1)} %concatenate.127.refs_0_, bf16[288,512]{1,0:T(8,128)(2,1)} %slice.300.refs_1_, bf16[288,512]{1,0:T(8,128)(2,1)} %slice.377.refs_2_), custom_call_target="tpu_custom_call" | custom-call | tf_op jit(solution)/shard_map/gather/pallas_call | solution.py:306
  152.6 4.4 slice_bitcast_fusion.3
  165.4 2.6 fusion.162
  170.3 2.4 fusion.160
  176.8 2.8 concatenate.137
  179.7 2.2 concatenate.139
  183.7 8.4 %collective-permute-done.2 = bf16[128,1152]{1,0:T(8,128)(2,1)S(1)} collective-permute-done((bf16[128,1152]{1,0:T(8,128)(2,1)}, bf16[128,1152]{1,0:T(8,128)(2,1)S(1)}, u32[]{:S(2)}, u32[]{:S(2)}) %collective-permute-start.2) | collective-permute-done | bytes 294944 | tf_op jit(solution)/shard_map/ppermute | solution.py:80
  193.8 2.5 fusion.7.x_ref
  196.3 27.8 %attend.1 = (bf16[4,896,432]{2,1,0:T(8,128)(2,1)}, bf16[4,896,144]{2,1,0:T(8,128)(2,1)}, f32[4,896,2]{2,1,0:T(8,128)}, f32[896,1152]{1,0:T(8,128)}) custom-call(bf16[896,1152]{1,0:T(8,128)(2,1)} %fusion.7.x_ref, bf16[4,1152,640]{2,1,0:T(8,128)(2,1)} %get-tuple-element.22.w_ref, f32[4,1,432]{2,1,0:T(1,128)} %broadcast_in_dim.62.b_ref, ...), custom_call_target="tpu_custom_call" | custom-call | flops 11333009408 | bytes 16220160 | tf_op jit(solution)/shard_map/attend/pallas_call | solution.py:569
  224.1 2.4 convert_element_type.173
  226.6 1.7 select_bitcast_fusion.1
  228.9 15.0 %collective-permute-done.9 = bf16[128,1152]{1,0:T(8,128)(2,1)S(1)} collective-permute-done((bf16[128,1152]{1,0:T(8,128)(2,1)S(1)}, bf16[128,1152]{1,0:T(8,128)(2,1)S(1)}, u32[]{:S(2)}, u32[]{:S(2)}) %collective-permute-start.9) | collective-permute-done | bytes 294944 | tf_op jit(solution)/shard_map/ppermute | solution.py:80
  243.9 1.6 convert_reduce_fusion.1
  253.9 1.8 fusion.84
  255.6 3.3 fusion.170
  258.9 3.3 fusion.173
  263.8 3.5 fusion.172
  268.8 3.3 fusion.171
  272.2 2.6 fusion.26
  274.7 2.6 fusion.25
  278.7 2.5 fusion.31
  282.6 1.9 convolution_add_fusion.5
  285.9 2.7 convolution_add_fusion.4
  302.0 1.6 fusion.30
  303.7 2.5 pad_maximum_fusion.1.refs_0_
  307.6 2.5 pad_maximum_fusion.2.refs_1_
  310.1 2.0 multiply_reduce_fusion
  312.2 3.5 fusion.155
  315.8 1.7 convert_element_type.196.r_ref
  318.4 45.8 %attend_back.1 = (bf16[4,896,432]{2,1,0:T(8,128)(2,1)}, f32[4,2,144]{2,1,0:T(2,128)}) custom-call(bf16[896,1152]{1,0:T(8,128)(2,1)} %convert_element_type.196.r_ref, bf16[4,1152,640]{2,1,0:T(8,128)(2,1)} %get-tuple-element.22.w_ref, bf16[4,896,432]{2,1,0:T(8,128)(2,1)} %get-tuple-element.26.qkv_ref, bf16[4,896,144]{2,1,0:T(8,128)(2,1)} %get-tuple-element.27.ctx_ref, ...), custom_call_target="tpu_custom_call" | custom-call | flops 17630756864 | bytes 16220160 | tf_op jit(solution)/shard_map/attend_back/pallas_call | solution.py:644
  364.2 2.7 fusion.56
  367.1 2.3 convolution_convert_fusion.8
  370.8 2.3 convolution_convert_fusion.9
  373.7 2.3 convolution_convert_fusion.10
  380.4 2.7 fusion.20
  385.2 1.7 copy.91
  387.0 2.1 copy.92
  389.1 2.4 copy.89
  392.6 1.8 copy.87
  395.4 3.1 convolution_convert_fusion.11
  398.5 1.6 copy.85
  400.1 2.3 convolution_convert_fusion.15
  403.6 2.8 concatenate.150
  406.3 2.9 concatenate.149
  409.2 4.1 concatenate.148
  413.4 4.0 concatenate.147
  417.4 5.0 pad_maximum_fusion.refs_2_
  422.4 151.7 %reduce.17 = (f32[288,512]{1,0:T(8,128)}, f32[288,512]{1,0:T(8,128)}, f32[288,640]{1,0:T(8,128)}) custom-call(bf16[4,1152,512]{2,1,0:T(8,128)(2,1)} %pad_maximum_fusion.1.refs_0_, bf16[4,1152,512]{2,1,0:T(8,128)(2,1)} %pad_maximum_fusion.2.refs_1_, bf16[4,1152,640]{2,1,0:T(8,128)(2,1)} %pad_maximum_fusion.refs_2_), custom_call_target="tpu_custom_call" | custom-call | tf_op jit(solution)/shard_map/reduce/pallas_call | solution.py:516
  575.4 2.0 pad_maximum_fusion.4
  577.4 1.8 slice_bitcast_fusion.4
  579.3 4.3 fusion.13
  584.8 2.0 maximum_bitcast_fusion.2
  587.9 1.8 copy.94
  592.9 2.8 collective-permute-done.15
  595.8 4.0 collective-permute-done.16
  601.1 4.6 fusion.12
  607.0 1.8 collective-permute-start.12
  610.8 7.1 %collective-permute-done.12 = bf16[128,1152]{1,0:T(8,128)(2,1)S(1)} collective-permute-done((bf16[128,1152]{1,0:T(8,128)(2,1)S(1)}, bf16[128,1152]{1,0:T(8,128)(2,1)S(1)}, u32[]{:S(2)}, u32[]{:S(2)}) %collective-permute-start.12) | collective-permute-done | bytes 294944 | tf_op jit(solution)/shard_map/ppermute | solution.py:80
  617.9 5.8 slice_select_fusion
  623.9 2.1 collective-permute-start.13
  626.7 6.9 %collective-permute-done.6 = bf16[192,1152]{1,0:T(8,128)(2,1)S(1)} collective-permute-done((bf16[192,1152]{1,0:T(8,128)(2,1)S(1)}, bf16[192,1152]{1,0:T(8,128)(2,1)S(1)}, u32[]{:S(2)}, u32[]{:S(2)}) %collective-permute-start.6) | collective-permute-done | bytes 442400 | tf_op jit(solution)/shard_map/ppermute | solution.py:80
  634.6 3.7 collective-permute-done.13
  (336 shorter events, 82.6 us)
Async XLA Ops:
  0.6 5.3 copy-start.35
  0.7 6.3 copy-start.36
  0.7 7.0 %copy-start.37 = (bf16[538,288]{0,1:T(8,128)(2,1)S(1)}, bf16[538,288]{0,1:T(8,128)(2,1)}, u32[]{:S(2)}) copy-start(bf16[538,288]{0,1:T(8,128)(2,1)} %param.20) | copy-start | bytes 929668
  2.8 5.7 copy-start.57
  2.8 7.5 %copy-start.38 = (bf16[3,288,144]{1,2,0:T(8,128)(2,1)S(1)}, bf16[3,288,144]{1,2,0:T(8,128)(2,1)}, u32[]{:S(2)}) copy-start(bf16[3,288,144]{1,2,0:T(8,128)(2,1)} %param.15) | copy-start | bytes 746500
  2.8 7.7 %copy-start.42 = (bf16[144,288]{1,0:T(8,128)(2,1)S(1)}, bf16[144,288]{1,0:T(8,128)(2,1)}, u32[]{:S(2)}) copy-start(bf16[144,288]{1,0:T(8,128)(2,1)} %param.17) | copy-start | bytes 248836
  2.8 7.8 %copy-start.58 = (f32[2,144]{1,0:T(2,128)S(1)}, f32[2,144]{1,0:T(2,128)}, u32[]{:S(2)}) copy-start(f32[2,144]{1,0:T(2,128)} %param.16) | copy-start | bytes 3460
  2.8 8.0 %copy-start.63 = (bf16[538]{0:T(1024)(128)(2,1)S(1)}, bf16[538]{0:T(1024)(128)(2,1)}, u32[]{:S(2)}) copy-start(bf16[538]{0:T(1024)(128)(2,1)} %param.19) | copy-start | bytes 3232
  2.8 8.3 %slice-start.6 = ((bf16[288,538]{1,0:T(8,128)(2,1)}), bf16[288,26]{1,0:T(8,128)(2,1)S(1)}, s32[]{:S(2)}) async-start(bf16[288,538]{1,0:T(8,128)(2,1)} %param.18), calls=%async_computation.6 | async-start | bytes 147456 | tf_op jit(solution)/shard_map/slice | solution.py:761
  2.8 179.0 %collective-permute-start.7 = (bf16[192,1152]{1,0:T(8,128)(2,1)}, bf16[192,1152]{1,0:T(8,128)(2,1)}, u32[]{:S(2)}, u32[]{:S(2)}) collective-permute-start(bf16[192,1152]{1,0:T(8,128)(2,1)} %get-tuple-element.124), channel_id=1, source_target_pairs={{0,2},{2,0},{4,6},{6,4},{1,3},{3,1},{5,7},{7,5},{8,10},{10,8},{12,... | collective-permute-start | bytes 1327112 | tf_op jit(solution)/shard_map/ppermute | solution.py:80
  6.9 161.0 %collective-permute-start = (bf16[192,1152]{1,0:T(8,128)(2,1)}, bf16[192,1152]{1,0:T(8,128)(2,1)}, u32[]{:S(2)}, u32[]{:S(2)}) collective-permute-start(bf16[192,1152]{1,0:T(8,128)(2,1)} %get-tuple-element.126), channel_id=1, source_target_pairs={{0,2},{2,0},{4,6},{6,4},{1,3},{3,1},{5,7},{7,5},{8,10},{10,8},{12,... | collective-permute-start | bytes 1327112 | tf_op jit(solution)/shard_map/ppermute | solution.py:80
  157.0 11.0 %copy-start.10 = (bf16[1152,640]{1,0:T(8,128)(2,1)}, bf16[1152,640]{1,0:T(8,128)(2,1)S(1)}, u32[]{:S(2)}) copy-start(bf16[1152,640]{1,0:T(8,128)(2,1)S(1)} %get-tuple-element.105) | copy-start | bytes 4423684
  157.0 13.3 %copy-start.8 = (bf16[1152,640]{1,0:T(8,128)(2,1)}, bf16[1152,640]{1,0:T(8,128)(2,1)S(1)}, u32[]{:S(2)}) copy-start(bf16[1152,640]{1,0:T(8,128)(2,1)S(1)} %get-tuple-element.104) | copy-start | bytes 4423684
  157.0 6.8 %copy-start.51 = (f32[4,1152]{1,0:T(4,128)S(1)}, f32[4,1152]{1,0:T(4,128)}, u32[]{:S(2)}) copy-start(f32[4,1152]{1,0:T(4,128)} %param.14) | copy-start | bytes 55300
  157.0 6.8 %copy-start.54 = (f32[2,1152]{1,0:T(2,128)S(1)}, f32[2,1152]{1,0:T(2,128)}, u32[]{:S(2)}) copy-start(f32[2,1152]{1,0:T(2,128)} %param.13) | copy-start | bytes 27652
  163.8 4.1 copy-start.14
  163.9 29.3 %copy-start.40 = (f32[1152]{0:T(1024)}, f32[1152]{0:T(1024)S(1)}, u32[]{:S(2)}) copy-start(f32[1152]{0:T(1024)S(1)} %get-tuple-element.157) | copy-start | bytes 13828
  169.3 3.4 collective-permute-start.1
  174.5 71.6 %copy-start = (bf16[2,2,192,1152]{3,2,1,0:T(8,128)(2,1)}, bf16[2,2,192,1152]{3,2,1,0:T(8,128)(2,1)S(1)}, u32[]{:S(2)}) copy-start(bf16[2,2,192,1152]{3,2,1,0:T(8,128)(2,1)S(1)} %copy.77) | copy-start | bytes 5308420
  174.5 5.1 copy-start.29
  174.5 5.1 copy-start.30
  175.3 16.8 %collective-permute-start.2 = (bf16[128,1152]{1,0:T(8,128)(2,1)}, bf16[128,1152]{1,0:T(8,128)(2,1)S(1)}, u32[]{:S(2)}, u32[]{:S(2)}) collective-permute-start(bf16[128,1152]{1,0:T(8,128)(2,1)} %pad_maximum_fusion.5), channel_id=1, source_target_pairs={{0,4},{2,6},{4,0},{6,2},{1,5},{3,7},{5,1},{7,3},{8,12},{10,14},{12... | collective-permute-start | bytes 884744 | tf_op jit(solution)/shard_map/ppermute | solution.py:80
  183.2 43.4 %collective-permute-start.8 = (bf16[2,192,1152]{2,1,0:T(8,128)(2,1)S(1)}, bf16[2,192,1152]{2,1,0:T(8,128)(2,1)}, u32[]{:S(2)}, u32[]{:S(2)}) collective-permute-start(bf16[2,192,1152]{2,1,0:T(8,128)(2,1)S(1)} %maximum_select_fusion.5), channel_id=1, source_target_pairs={{0,1},{1,0},{2,3},{3,2},{4,5},{5,4},{6,7},{7,6},{8,9},{9,8},{10,11... | collective-permute-start | bytes 2654216 | tf_op jit(solution)/shard_map/ppermute | solution.py:76
  192.2 54.0 %copy-start.4 = (bf16[128,1152]{1,0:T(8,128)(2,1)}, bf16[128,1152]{1,0:T(8,128)(2,1)S(1)}, u32[]{:S(2)}) copy-start(bf16[128,1152]{1,0:T(8,128)(2,1)S(1)} %collective-permute-done.2) | copy-start | bytes 884740
  226.5 19.6 %collective-permute-start.3 = (bf16[896,1152]{1,0:T(8,128)(2,1)S(1)}, bf16[896,1152]{1,0:T(8,128)(2,1)S(1)}, u32[]{:S(2)}, u32[]{:S(2)}) collective-permute-start(bf16[896,1152]{1,0:T(8,128)(2,1)S(1)} %convert_element_type.173), channel_id=1, source_target_pairs={{0,1},{1,0},{2,3},{3,2},{4,5},{5,4},{6,7},{7,6},{8,9},{9,8},{10,11... | collective-permute-start | bytes 6193160 | tf_op jit(solution)/shard_map/ppermute | solution.py:76
  228.7 15.2 %collective-permute-start.9 = (bf16[128,1152]{1,0:T(8,128)(2,1)S(1)}, bf16[128,1152]{1,0:T(8,128)(2,1)S(1)}, u32[]{:S(2)}, u32[]{:S(2)}) collective-permute-start(bf16[128,1152]{1,0:T(8,128)(2,1)S(1)} %pad_maximum_fusion.6), channel_id=1, source_target_pairs={{0,4},{2,6},{4,0},{6,2},{1,5},{3,7},{5,1},{7,3},{8,12},{10,14},{12... | collective-permute-start | bytes 884744 | tf_op jit(solution)/shard_map/ppermute | solution.py:80
  228.9 16.7 %copy-start.52 = (pred[896]{0:T(1024)(128)(4,1)}, pred[896]{0:T(1024)(128)(4,1)S(1)}, u32[]{:S(2)}) copy-start(pred[896]{0:T(1024)(128)(4,1)S(1)} %and_or_fusion) | copy-start | bytes 2692
  228.9 17.3 %copy-start.3 = (f32[896,1152]{1,0:T(8,128)S(1)}, f32[896,1152]{1,0:T(8,128)}, u32[]{:S(2)}) copy-start(f32[896,1152]{1,0:T(8,128)} %get-tuple-element.23) | copy-start | bytes 12386308
  243.9 4.4 slice-start.2
  258.9 18.4 %copy-start.66 = (bf16[896,512]{1,0:T(8,128)(2,1)}, bf16[896,512]{1,0:T(8,128)(2,1)S(1)}, u32[]{:S(2)}) copy-start(bf16[896,512]{1,0:T(8,128)(2,1)S(1)} %get-tuple-element.150) | copy-start | bytes 2752516
  272.2 9.0 %copy-start.33 = (bf16[896,512]{1,0:T(8,128)(2,1)}, bf16[896,512]{1,0:T(8,128)(2,1)S(1)}, u32[]{:S(2)}) copy-start(bf16[896,512]{1,0:T(8,128)(2,1)S(1)} %get-tuple-element.152) | copy-start | bytes 2752516
  293.3 16.8 %collective-permute-start.10 = (bf16[896,1152]{1,0:T(8,128)(2,1)S(1)}, bf16[896,1152]{1,0:T(8,128)(2,1)S(1)}, u32[]{:S(2)}, u32[]{:S(2)}) collective-permute-start(bf16[896,1152]{1,0:T(8,128)(2,1)S(1)} %fusion.22), channel_id=1, source_target_pairs={{0,1},{1,0},{2,3},{3,2},{4,5},{5,4},{6,7},{7,6},{8,9},{9,8},{10,11... | collective-permute-start | bytes 6193160 | tf_op jit(solution)/shard_map/ppermute | solution.py:76
  299.0 13.2 %collective-permute-start.4 = (bf16[896,1152]{1,0:T(8,128)(2,1)S(1)}, bf16[896,1152]{1,0:T(8,128)(2,1)S(1)}, u32[]{:S(2)}, u32[]{:S(2)}) collective-permute-start(bf16[896,1152]{1,0:T(8,128)(2,1)S(1)} %fusion.21), channel_id=1, source_target_pairs={{0,1},{1,0},{2,3},{3,2},{4,5},{5,4},{6,7},{7,6},{8,9},{9,8},{10,11... | collective-permute-start | bytes 6193160 | tf_op jit(solution)/shard_map/ppermute | solution.py:76
  315.8 67.4 %copy-start.6 = (bf16[896,1152]{1,0:T(8,128)(2,1)}, bf16[896,1152]{1,0:T(8,128)(2,1)S(1)}, u32[]{:S(2)}) copy-start(bf16[896,1152]{1,0:T(8,128)(2,1)S(1)} %get-tuple-element.106) | copy-start | bytes 6193156
  318.4 45.8 %copy-start.15 = (bf16[1152,640]{1,0:T(8,128)(2,1)S(1)}, bf16[1152,640]{1,0:T(8,128)(2,1)}, u32[]{:S(2)}) copy-start(bf16[1152,640]{1,0:T(8,128)(2,1)} %get-tuple-element.102) | copy-start | bytes 4423684
  380.4 4.2 copy-start.47
  380.4 4.8 copy-start.56
  383.1 196.2 %collective-permute-start.11 = (bf16[896,1152]{1,0:T(8,128)(2,1)}, bf16[896,1152]{1,0:T(8,128)(2,1)}, u32[]{:S(2)}, u32[]{:S(2)}) collective-permute-start(bf16[896,1152]{1,0:T(8,128)(2,1)} %fusion.20), channel_id=1, source_target_pairs={{0,1},{1,0},{2,3},{3,2},{4,5},{5,4},{6,7},{7,6},{8,9},{9,8},{10,11... | collective-permute-start | bytes 6193160 | tf_op jit(solution)/shard_map/ppermute | solution.py:76
  384.0 205.8 %collective-permute-start.5 = (bf16[128,1152]{1,0:T(8,128)(2,1)}, bf16[128,1152]{1,0:T(8,128)(2,1)}, u32[]{:S(2)}, u32[]{:S(2)}) collective-permute-start(bf16[128,1152]{1,0:T(8,128)(2,1)} %slice.401), channel_id=1, source_target_pairs={{0,4},{2,6},{4,0},{6,2},{1,5},{3,7},{5,1},{7,3},{8,12},{10,14},{12... | collective-permute-start | bytes 884744 | tf_op jit(solution)/shard_map/ppermute | solution.py:80
  387.0 5.6 copy-start.32
  409.2 4.2 copy-start.26
  574.1 5.2 copy-start.1
  574.1 5.2 copy-start.5
  574.1 5.2 copy-start.41
  574.1 5.2 copy-start.44
  574.1 5.2 copy-start.46
  579.2 4.4 copy-start.48
  579.2 4.5 copy-start.49
  579.2 4.5 copy-start.50
  579.2 4.5 copy-start.39
  579.2 4.6 copy-start.61
  579.2 4.6 copy-start.62
  579.2 4.6 copy-start.60
  579.3 4.6 copy-start.59
  579.3 4.6 copy-start.64
  583.9 7.6 %collective-permute-start.14 = (f32[80,128]{1,0:T(8,128)S(1)}, f32[80,128]{1,0:T(8,128)S(1)}, u32[]{:S(2)}, u32[]{:S(2)}) collective-permute-start(f32[80,128]{1,0:T(8,128)S(1)} %bitcast.260), channel_id=1, source_target_pairs={{0,8},{8,0},{1,9},{9,1},{2,10},{10,2},{3,11},{11,3},{4,12},{12,4},... | collective-permute-start | bytes 122888 | tf_op jit(solution)/shard_map/ppermute | solution.py:76
  591.6 4.1 collective-permute-start.15
  595.7 4.1 collective-permute-start.16
  599.7 18.1 %copy-start.53 = (pred[896]{0:T(1024)(128)(4,1)S(1)}, pred[896]{0:T(1024)(128)(4,1)}, u32[]{:S(2)}) copy-start(pred[896]{0:T(1024)(128)(4,1)} %copy-done.52) | copy-start | bytes 2692
  599.8 18.1 %copy-start.55 = (bf16[768]{0:T(1024)(128)(2,1)S(1)}, bf16[768]{0:T(1024)(128)(2,1)}, u32[]{:S(2)}) copy-start(bf16[768]{0:T(1024)(128)(2,1)} %pad.52.clone) | copy-start | bytes 4612
  599.8 9.0 %collective-permute-start.17 = (f32[80,128]{1,0:T(8,128)S(1)}, f32[80,128]{1,0:T(8,128)S(1)}, u32[]{:S(2)}, u32[]{:S(2)}) collective-permute-start(f32[80,128]{1,0:T(8,128)S(1)} %add.356), channel_id=1, source_target_pairs={{0,4},{2,6},{4,0},{6,2},{1,5},{3,7},{5,1},{7,3},{8,12},{10,14},{12... | collective-permute-start | bytes 122888 | tf_op jit(solution)/shard_map/ppermute | solution.py:80
  607.0 10.8 %collective-permute-start.12 = (bf16[128,1152]{1,0:T(8,128)(2,1)S(1)}, bf16[128,1152]{1,0:T(8,128)(2,1)S(1)}, u32[]{:S(2)}, u32[]{:S(2)}) collective-permute-start(bf16[128,1152]{1,0:T(8,128)(2,1)S(1)} %slice.412), channel_id=1, source_target_pairs={{0,4},{2,6},{4,0},{6,2},{1,5},{3,7},{5,1},{7,3},{8,12},{10,14},{12... | collective-permute-start | bytes 884744 | tf_op jit(solution)/shard_map/ppermute | solution.py:80
  623.8 9.8 %collective-permute-start.6 = (bf16[192,1152]{1,0:T(8,128)(2,1)S(1)}, bf16[192,1152]{1,0:T(8,128)(2,1)S(1)}, u32[]{:S(2)}, u32[]{:S(2)}) collective-permute-start(bf16[192,1152]{1,0:T(8,128)(2,1)S(1)} %get-tuple-element.112), channel_id=1, source_target_pairs={{0,2},{2,0},{4,6},{6,4},{1,3},{3,1},{5,7},{7,5},{8,10},{10,8},{12,... | collective-permute-start | bytes 1327112 | tf_op jit(solution)/shard_map/ppermute | solution.py:80
  623.9 14.4 %collective-permute-start.13 = (bf16[192,1152]{1,0:T(8,128)(2,1)S(1)}, bf16[192,1152]{1,0:T(8,128)(2,1)S(1)}, u32[]{:S(2)}, u32[]{:S(2)}) collective-permute-start(bf16[192,1152]{1,0:T(8,128)(2,1)S(1)} %get-tuple-element.108), channel_id=1, source_target_pairs={{0,2},{2,0},{4,6},{6,4},{1,3},{3,1},{5,7},{7,5},{8,10},{10,8},{12,... | collective-permute-start | bytes 1327112 | tf_op jit(solution)/shard_map/ppermute | solution.py:80
  (29 other events, 65.6 us)
